TPU v7x, 32 devices: a whole 2x2x4 slice. The times are simulated.
32 devices in a mesh: seq: 16 (over z, x, core), head: 2 (over y).
Axes of the slice: x: 2, y: 2, z: 4, core: 2. Of those that a mesh axis runs over, the one named last changes fastest.
Arguments:
- hidden: bfloat16 [4608, 8192], P('seq'), may hold values from -6 to 6
- norm_gain: bfloat16 [8192], replicated, may hold values from 0.099609375 to 1.8984375
- w_query: bfloat16 [8192, 1024], P('seq', 'head'), may hold values from -0.125 to 0.125
- w_key: bfloat16 [8192, 256], P('seq', 'head'), may hold values from -0.125 to 0.125
- w_value: bfloat16 [8192, 256], P('seq', 'head'), may hold values from -0.0625 to 0.0625
- bias_query: bfloat16 [1024], P('head'), may hold values from -3 to 3
- bias_key: bfloat16 [256], P('head'), may hold values from -200 to 200
- bias_value: bfloat16 [256], P('head'), may hold values from -3 to 3
- w_out: bfloat16 [1024, 8192], P('head', 'seq'), may hold values from -0.1875 to 0.1875
Outputs:
- attn_out: bfloat16 [4608, 8192], P(('seq', 'head'))
All inputs are finite; a program needn't handle non-finite values.
Results may differ from a plain program's by a relative error of at most 0.014.
The roundings to bfloat16 on the way count: a program that leaves them out, or rounds other values in their place, can miss the bound.
Values may be sent and summed in bfloat16 or wider, within the bound.
A program may use at most 192 MiB of HBM per device.

v0:
```python
import functools

import jax
import jax.numpy as jnp
import numpy as np
from jax import lax
from jax.experimental import pallas as pl
from jax.experimental.pallas import tpu as pltpu
from jax.sharding import PartitionSpec as P

HEAD_DIM = 128
ROPE_BASE = 1000000.0
EPSILON = 1e-06
MESH = pl.DeviceIdType.MESH
F32 = jnp.float32
BF16 = jnp.bfloat16


def kernel(
    n, groups, exchange,
    hidden, w_query, w_key, w_value, w_out, gain, bias_query, bias_key, bias_value,
    near_cos, near_sin, far_cos, far_sin,
    out,
    hid, w_all, wo_all, acc, kv_all, q_ref, high, total, mixed, att, ts, tr, tm,
    load_sem, ws, wr, wps, wpr, os_, or_, ops, opr, ks, kr, kps, kpr, ys, yr,
):
    chips = n // 2
    depth = chips // 2
    me = lax.axis_index("seq")
    group = lax.axis_index("head")
    core = me % 2
    chip = me // 2
    ring = chip // 2 + (chip % 2) * (2 * depth - 1 - 2 * (chip // 2))

    def device_at(position, which):
        position = (position + 2 * chips) % chips
        side = position // depth
        row = position + side * (2 * depth - 1 - 2 * position)
        return 2 * (2 * row + side) + which

    right = device_at(ring + 1, core)
    left = device_at(ring - 1, core)
    partner = 2 * chip + (1 - core)
    neighbours = (right, left)

    def source_at(direction, offset, which):
        return device_at(ring - offset if direction == 0 else ring + offset, which)

    rows, width = hidden.shape
    half_depth = w_query.shape[0] // 2
    q_cols = w_query.shape[1]
    heads = q_cols // HEAD_DIM
    half_cols = w_out.shape[1] // 2
    rh = rows // groups

    loads = []
    late = [pltpu.make_async_copy(hidden, hid, load_sem.at[0])]
    for h in range(2):
        span = pl.ds(h * half_depth, half_depth)
        slot = w_all.at[2 * me + h]
        loads.append(pltpu.make_async_copy(w_query.at[span], slot.at[:, pl.ds(0, q_cols)], load_sem.at[1 + 4 * h]))
        loads.append(pltpu.make_async_copy(w_key.at[span], slot.at[:, pl.ds(q_cols, HEAD_DIM)], load_sem.at[2 + 4 * h]))
        loads.append(pltpu.make_async_copy(w_value.at[span], slot.at[:, pl.ds(q_cols + HEAD_DIM, HEAD_DIM)], load_sem.at[3 + 4 * h]))
        late.append(pltpu.make_async_copy(w_out.at[:, pl.ds(h * half_cols, half_cols)], wo_all.at[2 * me + h], load_sem.at[4 + 4 * h]))
    for copy in loads + late:
        copy.start()

    barrier = pltpu.get_barrier_semaphore()
    for device in (right, left, partner):
        pl.semaphore_signal(barrier, inc=1, device_id={"seq": device}, device_id_type=MESH)
    peers = range(1, groups) if exchange else ()
    for p in peers:
        pl.semaphore_signal(barrier, inc=1, device_id={"head": (group + p) % groups}, device_id_type=MESH)
    pl.semaphore_wait(barrier, 3 + len(peers))

    def remote(ref, send, recv, key, device):
        return pltpu.make_async_remote_copy(
            src_ref=ref, dst_ref=ref, send_sem=send.at[key], recv_sem=recv.at[key],
            device_id={"seq": device}, device_id_type=MESH,
        )

    def piece(buffer, index, j):
        size = buffer.shape[1] // 2
        return buffer.at[index, pl.ds(j * size, size)]

    def key_of(direction, step, j):
        return (direction * chips + step) * 2 + j

    def ring_begin(buffer, sems):
        ss, rs, pss, prs = sems
        for j in range(2):
            for d in range(2):
                own = piece(buffer, 2 * me + d, j)
                remote(own, ss, rs, key_of(d, 0, j), neighbours[d]).start()
        for j in range(2):
            for d in range(2):
                own = piece(buffer, 2 * me + d, j)
                remote(own, pss, prs, key_of(d, chips - 1, j), partner).start()

    def ring_advance(buffer, sems, t):
        ss, rs, pss, prs = sems

        @pl.when(t < chips - 1)
        def _():
            for j in range(2):
                for d in range(2):
                    block = piece(buffer, 2 * source_at(d, t + 1, core) + d, j)
                    remote(block, ss, rs, key_of(d, t, j), neighbours[d]).wait_recv()

                    @pl.when(t < chips - 2)
                    def _():
                        remote(block, ss, rs, key_of(d, t + 1, j), neighbours[d]).start()

                    remote(block, pss, prs, key_of(d, t, j), partner).start()

    def partner_wait(buffer, sems, t):
        ss, rs, pss, prs = sems
        for j in range(2):
            for d in range(2):
                block = piece(buffer, 2 * source_at(d, t, 1 - core) + d, j)
                remote(block, pss, prs, key_of(d, (t + chips - 1) % chips, j), partner).wait_recv()

    def ring_drain(buffer, sems):
        ss, rs, pss, prs = sems

        def body(t, carry):
            for j in range(2):
                for d in range(2):
                    block = piece(buffer, 2 * me + d, j)

                    @pl.when(t < chips - 1)
                    def _():
                        remote(block, ss, rs, key_of(d, t, j), neighbours[d]).wait_send()

                    remote(block, pss, prs, key_of(d, t, j), partner).wait_send()
            return carry

        lax.fori_loop(0, chips, body, 0)

    w_sems = (ws, wr, wps, wpr)
    o_sems = (os_, or_, ops, opr)

    for copy in loads:
        copy.wait()
    ring_begin(w_all, w_sems)
    for copy in late:
        copy.wait()
    slices = 2 * n
    step_cols = width // slices

    def columns(i):
        return pl.ds(pl.multiple_of(i * step_cols, step_cols), step_cols)

    def square(i, carry):
        x = hid[:, columns(i)].astype(F32)
        return carry + x * x

    squares = lax.fori_loop(0, slices, square, jnp.zeros((rows, step_cols), F32))
    inverse = lax.rsqrt(jnp.sum(squares, axis=-1, keepdims=True) * (1.0 / width) + EPSILON)

    def normed(i):
        scaled = hid[:, columns(i)].astype(F32) * inverse * gain[:, columns(i)].astype(F32)
        return scaled.astype(BF16)

    bias = (bias_query, bias_key, bias_value)
    starts = (0, q_cols, q_cols + HEAD_DIM)
    for start, part in zip(starts, bias):
        span = pl.ds(start, part.shape[1])
        acc[:, span] = jnp.broadcast_to(part[...].astype(F32), (rows, part.shape[1]))

    def project(t, carry):
        ring_advance(w_all, w_sems, t)
        partner_wait(w_all, w_sems, t)
        for d in range(2):
            i = 2 * source_at(d, t, core) + d
            k = 2 * source_at(d, t, 1 - core) + d
            acc[...] += jnp.dot(normed(i), w_all[i], preferred_element_type=F32) + jnp.dot(
                normed(k), w_all[k], preferred_element_type=F32
            )
        return carry

    lax.fori_loop(0, chips, project, 0)

    block_cos, block_sin = far_cos[me], far_sin[me]
    cosine = near_cos[...] * block_cos - near_sin[...] * block_sin
    lane = lax.broadcasted_iota(jnp.int32, cosine.shape, 1)
    sine = near_sin[...] * block_cos + near_cos[...] * block_sin
    sine = jnp.where(lane < HEAD_DIM // 2, -sine, sine)

    def rotary(x):
        return x * cosine + pltpu.roll(x, HEAD_DIM // 2, 1) * sine

    def kv_rows(which):
        return pl.ds(pl.multiple_of(which * rows, rows), rows)

    kv_all[chip, kv_rows(core), pl.ds(0, HEAD_DIM)] = rotary(acc[:, pl.ds(q_cols, HEAD_DIM)]).astype(BF16)
    kv_all[chip, kv_rows(core), pl.ds(HEAD_DIM, HEAD_DIM)] = acc[:, pl.ds(q_cols + HEAD_DIM, HEAD_DIM)].astype(BF16)
    for h in range(heads):
        q_ref[h] = rotary(acc[:, pl.ds(h * HEAD_DIM, HEAD_DIM)]).astype(BF16)

    reach = (chips // 2, chips - 1 - chips // 2)

    parts = 2 if rows % 32 == 0 else 1
    piece_rows = rows // parts

    def kv_copy(owner, ss, rs, direction, step, j, device):
        start = pl.multiple_of((owner % 2) * rows + j * piece_rows, piece_rows)
        block = kv_all.at[owner // 2, pl.ds(start, piece_rows)]
        return remote(block, ss, rs, key_of(direction, step, j), device)

    for j in range(parts):
        for d in range(2):
            kv_copy(me, ks, kr, d, 0, j, neighbours[d]).start()
        kv_copy(me, kps, kpr, 0, chips - 1, j, partner).start()

    factor = HEAD_DIM ** (-0.5) * 1.4426950408889634

    def attend(c, own):
        for h in range(heads):
            scores = lax.dot_general(
                q_ref[h], kv_all[c, :, pl.ds(0, HEAD_DIM)], (((1,), (1,)), ((), ())),
                preferred_element_type=F32,
            )
            if own:
                row = lax.broadcasted_iota(jnp.int32, scores.shape, 0) + core * rows
                col = lax.broadcasted_iota(jnp.int32, scores.shape, 1)
                scores = jnp.where(row >= col, scores, -jnp.inf)
            top = jnp.max(scores, axis=-1, keepdims=True)
            if not own:
                old = high[h]
                top = jnp.maximum(old, top)
            probs = jnp.exp2((scores - top) * factor)
            part = jnp.sum(probs, axis=-1, keepdims=True)
            product = jnp.dot(
                probs.astype(BF16), kv_all[c, :, pl.ds(HEAD_DIM, HEAD_DIM)], preferred_element_type=F32
            )
            if not own:
                shrink = jnp.exp2((old - top) * factor)
                part = part + total[h] * shrink
                product = product + mixed[h] * shrink
            high[h] = top
            total[h] = part
            mixed[h] = product

    for j in range(parts):
        kv_copy(partner, kps, kpr, 0, chips - 1, j, partner).wait_recv()
    attend(chip, True)

    def attention(t, carry):
        for j in range(parts):
            for d in range(2):
                @pl.when(t < reach[d])
                def _():
                    owner = source_at(d, t + 1, core)
                    kv_copy(owner, ks, kr, d, t, j, neighbours[d]).wait_recv()

                    @pl.when(t + 1 < reach[d])
                    def _():
                        kv_copy(owner, ks, kr, d, t + 1, j, neighbours[d]).start()

                    kv_copy(owner, kps, kpr, d, t, j, partner).start()

        @pl.when(t == reach[0] - 1)
        def _():
            ring_begin(wo_all, o_sems)

        for d in range(2):
            @pl.when((t > 0) & (t <= reach[d]))
            def _():
                owner = source_at(d, t, 1 - core)
                for j in range(parts):
                    kv_copy(owner, kps, kpr, d, t - 1, j, partner).wait_recv()

                @pl.when(owner // 2 < chip)
                def _():
                    attend(owner // 2, False)
        return carry

    lax.fori_loop(0, reach[0] + 1, attention, 0)
    for h in range(heads):
        att[:, pl.ds(h * HEAD_DIM, HEAD_DIM)] = (mixed[h] / total[h]).astype(BF16)

    def term_copy(p, i):
        return pltpu.make_async_remote_copy(
            src_ref=ts.at[p - 1, i], dst_ref=tr.at[p - 1, i],
            send_sem=ys.at[(p - 1) * slices + i], recv_sem=yr.at[(p - 1) * slices + i],
            device_id={"head": (group + p) % groups}, device_id_type=MESH,
        )

    def out_columns(i):
        return pl.ds(pl.multiple_of(i * half_cols, half_cols), half_cols)

    def make_term(i):
        if not exchange:
            out[:, out_columns(i)] = jnp.dot(att[...], wo_all[i], preferred_element_type=F32).astype(BF16)
            return
        for p in peers:
            span = pl.ds(pl.multiple_of(((group + p) % groups) * rh, rh), rh)
            ts[p - 1, i] = jnp.dot(att[span, :], wo_all[i], preferred_element_type=F32).astype(BF16)
            term_copy(p, i).start()
        span = pl.ds(pl.multiple_of(group * rh, rh), rh)
        tm[i] = jnp.dot(att[span, :], wo_all[i], preferred_element_type=F32).astype(BF16)

    def blocks_of(t):
        return [2 * source_at(d, t, which) + d for d in range(2) for which in (core, 1 - core)]

    def finish(t, carry):
        for i in blocks_of(t):
            value = tm[i].astype(F32)
            for p in peers:
                term_copy(p, i).wait_recv()
                value = value + tr[p - 1, i].astype(F32)
            out[:, out_columns(i)] = value.astype(BF16)
        return carry

    lag = 3

    def partner_terms(t):
        partner_wait(wo_all, o_sems, t)
        for d in range(2):
            make_term(2 * source_at(d, t, 1 - core) + d)

    for d in range(2):
        make_term(2 * me + d)
    partner_terms(0)

    def project_out(t, carry):
        ring_advance(wo_all, o_sems, t)

        @pl.when(t < chips - 1)
        def _():
            for d in range(2):
                make_term(2 * source_at(d, t + 1, core) + d)

        @pl.when(t > 0)
        def _():
            partner_terms(t)

        if exchange:
            @pl.when(t >= lag)
            def _():
                finish(t - lag, 0)
        return carry

    lax.fori_loop(0, chips, project_out, 0)

    if exchange:
        lax.fori_loop(chips - lag, chips, finish, 0)

        def sent(i, carry):
            for p in peers:
                term_copy(p, i).wait_send()
            return carry

        lax.fori_loop(0, slices, sent, 0)

    ring_drain(w_all, w_sems)
    ring_drain(wo_all, o_sems)
    for j in range(parts):
        for d in range(2):
            for t in range(reach[d]):
                kv_copy(me, ks, kr, d, t, j, neighbours[d]).wait_send()
                kv_copy(me, kps, kpr, d, t, j, partner).wait_send()
        kv_copy(me, kps, kpr, 0, chips - 1, j, partner).wait_send()


def local(n, groups, hidden, norm_gain, w_query, w_key, w_value, bias_query, bias_key, bias_value, w_out):
    rows, width = hidden.shape
    cols = w_query.shape[1]
    heads = cols // HEAD_DIM
    wide = cols + 2 * HEAD_DIM
    chips = n // 2
    exchange = groups > 1 and (rows // groups) % 16 == 0
    rh = rows // groups
    slices = 2 * n
    half_depth = w_query.shape[0] // 2
    half_cols = w_out.shape[1] // 2

    freq = ROPE_BASE ** (-2.0 * np.arange(HEAD_DIM // 2, dtype=np.float64) / HEAD_DIM)
    freq = np.concatenate([freq, freq])
    near = np.arange(rows, dtype=np.float64)[:, None] * freq
    far = (np.arange(n, dtype=np.float64) * rows)[:, None, None] * freq
    tables = [f(a).astype(np.float32) for a in (near, far) for f in (np.cos, np.sin)]
    vectors = [v.reshape(1, -1) for v in (norm_gain, bias_query, bias_key, bias_value)]

    any_spec = pl.BlockSpec(memory_space=pl.ANY)
    vmem = pl.BlockSpec(memory_space=pltpu.VMEM)
    links = max(groups - 1, 1) if exchange else 1
    pieces = slices if exchange else 1
    rpart = rh if exchange else 16
    dma = pltpu.SemaphoreType.DMA
    result = pl.pallas_call(
        functools.partial(kernel, n, groups, exchange),
        out_shape=jax.ShapeDtypeStruct((rh if exchange else rows, w_out.shape[1] * n), BF16),
        in_specs=[any_spec] * 5 + [vmem] * 8,
        out_specs=vmem,
        scratch_shapes=[
            pltpu.VMEM((rows, width), BF16),
            pltpu.VMEM((slices, half_depth, wide), BF16),
            pltpu.VMEM((slices, w_out.shape[0], half_cols), BF16),
            pltpu.VMEM((rows, wide), F32),
            pltpu.VMEM((chips, 2 * rows, 2 * HEAD_DIM), BF16),
            pltpu.VMEM((heads, rows, HEAD_DIM), BF16),
            pltpu.VMEM((heads, rows, 1), F32),
            pltpu.VMEM((heads, rows, 1), F32),
            pltpu.VMEM((heads, rows, HEAD_DIM), F32),
            pltpu.VMEM((rows, cols), BF16),
            pltpu.VMEM((links, pieces, rpart, half_cols), BF16),
            pltpu.VMEM((links, pieces, rpart, half_cols), BF16),
            pltpu.VMEM((pieces, rpart, half_cols), BF16),
            dma((9,)),
        ]
        + [dma((4 * chips,))] * 12
        + [dma((links * pieces,))] * 2,
        compiler_params=pltpu.CompilerParams(
            collective_id=0, has_side_effects=True, vmem_limit_bytes=64 * 1024 * 1024 - 128 * 1024
        ),
    )(hidden, w_query, w_key, w_value, w_out, *vectors, *tables)
    if exchange:
        return result
    return lax.psum_scatter(result, "head", scatter_dimension=0, tiled=True)


def solution(mesh):
    in_specs = (
        P("seq", None),
        P(),
        P("seq", "head"),
        P("seq", "head"),
        P("seq", "head"),
        P("head"),
        P("head"),
        P("head"),
        P("head", "seq"),
    )
    out_specs = P(("seq", "head"), None)
    body = functools.partial(local, mesh.shape["seq"], mesh.shape["head"])
    return jax.shard_map(body, mesh=mesh, in_specs=in_specs, out_specs=out_specs, check_vma=False)
```

profile of v0, /device:TPU:0, one launch (start us, length us, event | category | flops | bytes accessed | tf_op | source)
XLA Modules:
  0.0 153.5 jit_solution(10032460355386758714)
XLA Ops:
  0.0 1.3 reshape.13.bias_query
  1.3 1.3 reshape.12.gain
  2.6 147.6 %shard_map.127 = bf16[144,8192]{1,0:T(8,128)(2,1)} custom-call(bf16[288,8192]{1,0:T(8,128)(2,1)} %hidden.1, bf16[512,512]{1,0:T(8,128)(2,1)} %w_query.1, bf16[512,128]{1,0:T(8,128)(2,1)} %w_key.1, bf16[512,128]{1,0:T(8,128)(2,1)} %w_value.1, bf16[512,512]{1,0:T(8,128)(2,1)} %w_out.1, bf16[1,8192]{1,0:T(2,128)(2,1)} %reshape.12.gain, ...), custom_call_target="tpu_custom_call" | custom-call | tf_op jit(solution)/shard_map/pallas_call | solution.py:392
  150.2 3.3 %copy.15 = bf16[144,8192]{1,0:T(8,128)(2,1)} copy(bf16[144,8192]{1,0:T(8,128)(2,1)} %shard_map.127) | data formatting | bytes 4718592
where the time goes:
time: 156 us; the launch traced here: 153 us
  Pallas kernels  148 us (95%)
  local copies, waits for them, and re-layouts  5.9 us (4%)
    pallas_call x1, Pallas kernels, local(): pl.pallas_call(functools.partial(kernel, n, groups, exchange), out_shape=...  148 us
    unnamed x1, local copies, waits for them, and re-layouts  3.27 us

commit v1 on v0

--- a/solution.py
+++ b/solution.py
@@ -14,6 +14,7 @@
 MESH = pl.DeviceIdType.MESH
 F32 = jnp.float32
 BF16 = jnp.bfloat16
+VMEM_LIMIT = 48 * 1024 * 1024
 
 
 def kernel(
@@ -364,8 +365,504 @@
         kv_copy(me, kps, kpr, 0, chips - 1, j, partner).wait_send()
 
 
+def pair_kernel(
+    n, chunks_wide, chunks_narrow, chunks_out,
+    hidden, w_query, w_key, w_value, w_out, gain, bias_query, bias_key, bias_value,
+    near_cos, near_sin, far_cos, far_sin,
+    out,
+    hid, w_first, w_second, wo, acc_first, acc_second, kv_all, q_ref, high, total, mixed, att, terms,
+    load_sem, swap_s, swap_r, att_s, att_r, own_s, ys, yr,
+    fs, fr, fps, fpr, ss, sr, sps, spr, os_, or_, ops, opr, ks, kr, kps, kpr,
+):
+    chips = n // 2
+    depth = chips // 2
+    me = lax.axis_index("seq")
+    group = lax.axis_index("head")
+    peer = 1 - group
+    core = me % 2
+    chip = me // 2
+    ring = chip // 2 + (chip % 2) * (2 * depth - 1 - 2 * (chip // 2))
+
+    def device_at(position, which):
+        position = (position + 2 * chips) % chips
+        side = position // depth
+        row = position + side * (2 * depth - 1 - 2 * position)
+        return 2 * (2 * row + side) + which
+
+    right = device_at(ring + 1, core)
+    left = device_at(ring - 1, core)
+    partner = 2 * chip + (1 - core)
+    neighbours = (right, left)
+
+    def source_at(direction, offset, which):
+        return device_at(ring - offset if direction == 0 else ring + offset, which)
+
+    rows, width = hidden.shape
+    half_depth = w_query.shape[0] // 2
+    q_cols = w_query.shape[1]
+    heads = q_cols // HEAD_DIM
+    early = heads // 2
+    q_early = early * HEAD_DIM
+    q_late = q_cols - q_early
+    out_depth = w_out.shape[0]
+    group_cols = w_out.shape[1] // 2
+    lane_cols = group_cols // 2
+    rh = rows // 2
+
+    def remote(ref, send, recv, key, device):
+        return pltpu.make_async_remote_copy(
+            src_ref=ref, dst_ref=ref, send_sem=send.at[key], recv_sem=recv.at[key],
+            device_id={"seq": device}, device_id_type=MESH,
+        )
+
+    def lanes(which):
+        return pl.ds(pl.multiple_of(which * lane_cols, lane_cols), lane_cols)
+
+    def wo_lanes(which, d):
+        start = which * group_cols + d * lane_cols
+        return pl.ds(pl.multiple_of(start, lane_cols), lane_cols)
+
+    def group_rows(which):
+        return pl.ds(pl.multiple_of(which * out_depth, out_depth), out_depth)
+
+    loads, later, last = [], [], []
+    for h in range(2):
+        span = pl.ds(h * half_depth, half_depth)
+        slot = w_first.at[2 * me + h]
+        loads.append((w_key.at[span], slot.at[:, pl.ds(0, HEAD_DIM)]))
+        loads.append((w_value.at[span], slot.at[:, pl.ds(HEAD_DIM, HEAD_DIM)]))
+        loads.append((w_query.at[span, pl.ds(0, q_early)], slot.at[:, pl.ds(2 * HEAD_DIM, q_early)]))
+        later.append((w_query.at[span, pl.ds(q_early, q_late)], w_second.at[2 * me + h]))
+        last.append((w_out.at[:, wo_lanes(group, h)], wo.at[chip, h, group_rows(group), lanes(core)]))
+    later.append((hidden, hid))
+    copies = [pltpu.make_async_copy(a, b, load_sem.at[i]) for i, (a, b) in enumerate(loads + later + last)]
+    for copy in copies:
+        copy.start()
+
+    barrier = pltpu.get_barrier_semaphore()
+    for device in (right, left, partner):
+        pl.semaphore_signal(barrier, inc=1, device_id={"seq": device}, device_id_type=MESH)
+    pl.semaphore_signal(barrier, inc=1, device_id={"head": peer}, device_id_type=MESH)
+    pl.semaphore_wait(barrier, 4)
+
+    def across(src, dst, send, recv, key):
+        return pltpu.make_async_remote_copy(
+            src_ref=src, dst_ref=dst, send_sem=send.at[key], recv_sem=recv.at[key],
+            device_id={"head": peer}, device_id_type=MESH,
+        )
+
+    def swap(d):
+        return across(
+            w_out.at[:, wo_lanes(peer, d)], wo.at[chip, d, group_rows(group), lanes(core)], swap_s, swap_r, d
+        )
+
+    class Ring:
+        def __init__(self, view, sems, pieces):
+            self.view, self.sems, self.pieces = view, sems, pieces
+
+        def key(self, d, step, j):
+            return (d * chips + step) * self.pieces + j
+
+        def begin(self, j):
+            send, recv, psend, precv = self.sems
+            for d in range(2):
+                own = self.view(me, d, j)
+                remote(own, send, recv, self.key(d, 0, j), neighbours[d]).start()
+            for d in range(2):
+                own = self.view(me, d, j)
+                remote(own, psend, precv, self.key(d, chips - 1, j), partner).start()
+
+        def advance(self, t, j):
+            send, recv, psend, precv = self.sems
+            for d in range(2):
+                block = self.view(source_at(d, t + 1, core), d, j)
+                remote(block, send, recv, self.key(d, t, j), neighbours[d]).wait_recv()
+
+                @pl.when(t < chips - 2)
+                def _():
+                    remote(block, send, recv, self.key(d, t + 1, j), neighbours[d]).start()
+
+                remote(block, psend, precv, self.key(d, t, j), partner).start()
+
+        def partner_wait(self, t):
+            send, recv, psend, precv = self.sems
+            for j in range(self.pieces):
+                for d in range(2):
+                    block = self.view(source_at(d, t, 1 - core), d, j)
+                    remote(block, psend, precv, self.key(d, (t + chips - 1) % chips, j), partner).wait_recv()
+
+        def drain(self):
+            send, recv, psend, precv = self.sems
+
+            def body(t, carry):
+                for j in range(self.pieces):
+                    for d in range(2):
+                        block = self.view(me, d, j)
+
+                        @pl.when(t < chips - 1)
+                        def _():
+                            remote(block, send, recv, self.key(d, t, j), neighbours[d]).wait_send()
+
+                        remote(block, psend, precv, self.key(d, t, j), partner).wait_send()
+                return carry
+
+            lax.fori_loop(0, chips, body, 0)
+
+    def rows_view(buffer, pieces):
+        size = buffer.shape[1] // pieces
+        return lambda owner, d, j: buffer.at[2 * owner + d, pl.ds(pl.multiple_of(j * size, size), size)]
+
+    def wo_view(owner, d, j):
+        size = wo.shape[2] // chunks_out
+        return wo.at[owner // 2, d, pl.ds(pl.multiple_of(j * size, size), size), lanes(owner % 2)]
+
+    first = Ring(rows_view(w_first, chunks_wide), (fs, fr, fps, fpr), chunks_wide)
+    second = Ring(rows_view(w_second, chunks_narrow), (ss, sr, sps, spr), chunks_narrow)
+    third = Ring(wo_view, (os_, or_, ops, opr), chunks_out)
+
+    for copy in copies[: len(loads)]:
+        copy.wait()
+    for j in range(chunks_wide):
+        first.begin(j)
+    for d in range(2):
+        swap(d).start()
+    for copy in copies[len(loads):]:
+        copy.wait()
+
+    slices = 2 * n
+    step_cols = width // slices
+
+    def columns(i):
+        return pl.ds(pl.multiple_of(i * step_cols, step_cols), step_cols)
+
+    def square(i, carry):
+        x = hid[:, columns(i)].astype(F32)
+        return carry + x * x
+
+    squares = lax.fori_loop(0, slices, square, jnp.zeros((rows, step_cols), F32))
+    inverse = lax.rsqrt(jnp.sum(squares, axis=-1, keepdims=True) * (1.0 / width) + EPSILON)
+
+    def normed(i):
+        scaled = hid[:, columns(i)].astype(F32) * inverse * gain[:, columns(i)].astype(F32)
+        value = scaled.astype(BF16)
+        hid[:, columns(i)] = value
+        return value
+
+    def widen(value, size):
+        return jnp.broadcast_to(value.astype(F32), (rows, size))
+
+    acc_first[:, pl.ds(0, HEAD_DIM)] = widen(bias_key[...], HEAD_DIM)
+    acc_first[:, pl.ds(HEAD_DIM, HEAD_DIM)] = widen(bias_value[...], HEAD_DIM)
+    acc_first[:, pl.ds(2 * HEAD_DIM, q_early)] = widen(bias_query[:, pl.ds(0, q_early)], q_early)
+    acc_second[...] = widen(bias_query[:, pl.ds(q_early, q_late)], q_late)
+
+    def project_first(t, carry):
+        @pl.when(t < chips - 1)
+        def _():
+            for j in range(chunks_wide):
+                first.advance(t, j)
+
+        @pl.when(t == chips - 3)
+        def _():
+            for j in range(chunks_narrow):
+                second.begin(j)
+
+        first.partner_wait(t)
+        for d in range(2):
+            i = 2 * source_at(d, t, core) + d
+            k = 2 * source_at(d, t, 1 - core) + d
+            acc_first[...] += jnp.dot(normed(i), w_first[i], preferred_element_type=F32) + jnp.dot(
+                normed(k), w_first[k], preferred_element_type=F32
+            )
+        return carry
+
+    lax.fori_loop(0, chips, project_first, 0)
+
+    block_cos, block_sin = far_cos[me], far_sin[me]
+    cosine = near_cos[...] * block_cos - near_sin[...] * block_sin
+    lane = lax.broadcasted_iota(jnp.int32, cosine.shape, 1)
+    sine = near_sin[...] * block_cos + near_cos[...] * block_sin
+    sine = jnp.where(lane < HEAD_DIM // 2, -sine, sine)
+
+    def rotary(x):
+        return x * cosine + pltpu.roll(x, HEAD_DIM // 2, 1) * sine
+
+    def kv_rows(which):
+        return pl.ds(pl.multiple_of(which * rows, rows), rows)
+
+    kv_all[chip, kv_rows(core), pl.ds(0, HEAD_DIM)] = rotary(acc_first[:, pl.ds(0, HEAD_DIM)]).astype(BF16)
+    kv_all[chip, kv_rows(core), pl.ds(HEAD_DIM, HEAD_DIM)] = acc_first[:, pl.ds(HEAD_DIM, HEAD_DIM)].astype(BF16)
+    for h in range(early):
+        q_ref[h] = rotary(acc_first[:, pl.ds((2 + h) * HEAD_DIM, HEAD_DIM)]).astype(BF16)
+
+    reach = (chips // 2, chips - 1 - chips // 2)
+    parts = 2 if rows % 32 == 0 else 1
+    piece_rows = rows // parts
+
+    def kv_copy(owner, send, recv, direction, step, j, device):
+        start = pl.multiple_of((owner % 2) * rows + j * piece_rows, piece_rows)
+        block = kv_all.at[owner // 2, pl.ds(start, piece_rows)]
+        return remote(block, send, recv, (direction * chips + step) * parts + j, device)
+
+    for j in range(parts):
+        for d in range(2):
+            kv_copy(me, ks, kr, d, 0, j, neighbours[d]).start()
+        kv_copy(me, kps, kpr, 0, chips - 1, j, partner).start()
+    for j in range(chunks_narrow):
+        second.advance(0, j)
+
+    factor = HEAD_DIM ** (-0.5) * 1.4426950408889634
+
+    def attend(c, own, which):
+        for h in which:
+            scores = lax.dot_general(
+                q_ref[h], kv_all[c, :, pl.ds(0, HEAD_DIM)], (((1,), (1,)), ((), ())),
+                preferred_element_type=F32,
+            )
+            if own:
+                row = lax.broadcasted_iota(jnp.int32, scores.shape, 0) + core * rows
+                col = lax.broadcasted_iota(jnp.int32, scores.shape, 1)
+                scores = jnp.where(row >= col, scores, -jnp.inf)
+            top = jnp.max(scores, axis=-1, keepdims=True)
+            if not own:
+                old = high[h]
+                top = jnp.maximum(old, top)
+            probs = jnp.exp2((scores - top) * factor)
+            part = jnp.sum(probs, axis=-1, keepdims=True)
+            product = jnp.dot(
+                probs.astype(BF16), kv_all[c, :, pl.ds(HEAD_DIM, HEAD_DIM)], preferred_element_type=F32
+            )
+            if not own:
+                shrink = jnp.exp2((old - top) * factor)
+                part = part + total[h] * shrink
+                product = product + mixed[h] * shrink
+            high[h] = top
+            total[h] = part
+            mixed[h] = product
+
+    sooner, rest = range(early), range(early, heads)
+    for j in range(parts):
+        kv_copy(partner, kps, kpr, 0, chips - 1, j, partner).wait_recv()
+    attend(chip, True, sooner)
+
+    for d in range(2):
+        swap(d).wait_recv()
+
+    def attention(t, carry):
+        for j in range(parts):
+            for d in range(2):
+                @pl.when(t < reach[d])
+                def _():
+                    owner = source_at(d, t + 1, core)
+                    kv_copy(owner, ks, kr, d, t, j, neighbours[d]).wait_recv()
+
+                    @pl.when(t + 1 < reach[d])
+                    def _():
+                        kv_copy(owner, ks, kr, d, t + 1, j, neighbours[d]).start()
+
+                    kv_copy(owner, kps, kpr, d, t, j, partner).start()
+
+        @pl.when(t + 1 < chips - 1)
+        def _():
+            for j in range(chunks_narrow):
+                second.advance(t + 1, j)
+
+        for j in range(chunks_out):
+            @pl.when(t == min(reach[0] - 1 + j, chips - 3))
+            def _():
+                third.begin(j)
+
+        for d in range(2):
+            @pl.when((t > 0) & (t <= reach[d]))
+            def _():
+                owner = source_at(d, t, 1 - core)
+                for j in range(parts):
+                    kv_copy(owner, kps, kpr, d, t - 1, j, partner).wait_recv()
+
+                @pl.when(owner // 2 < chip)
+                def _():
+                    attend(owner // 2, False, sooner)
+
+        second.partner_wait(t)
+        for d in range(2):
+            i = 2 * source_at(d, t, core) + d
+            k = 2 * source_at(d, t, 1 - core) + d
+            acc_second[...] += jnp.dot(hid[:, columns(i)], w_second[i], preferred_element_type=F32) + jnp.dot(
+                hid[:, columns(k)], w_second[k], preferred_element_type=F32
+            )
+        return carry
+
+    lax.fori_loop(0, chips, attention, 0)
+
+    def head_span(which):
+        return pl.ds(which[0] * HEAD_DIM, len(which) * HEAD_DIM)
+
+    def att_copy(key, which):
+        ref = att.at[group, :, head_span(which)]
+        return across(ref, ref, att_s, att_r, key)
+
+    def settle(which):
+        for h in which:
+            att[group, :, pl.ds(h * HEAD_DIM, HEAD_DIM)] = (mixed[h] / total[h]).astype(BF16)
+
+    settle(sooner)
+    for h in rest:
+        q_ref[h] = rotary(acc_second[:, pl.ds((h - early) * HEAD_DIM, HEAD_DIM)]).astype(BF16)
+    att_copy(0, sooner).start()
+    attend(chip, True, rest)
+
+    def attention_rest(c, carry):
+        third.advance(c // chunks_out, c % chunks_out)
+
+        @pl.when(c < chip)
+        def _():
+            attend(c, False, rest)
+        return carry
+
+    lax.fori_loop(0, chips, attention_rest, 0)
+    settle(rest)
+    att_copy(1, rest).start()
+    lead = chips // chunks_out
+
+    def out_copy(c, d, which, key):
+        start = (2 * c + which) * 2 * group_cols + group * group_cols + d * lane_cols
+        span = pl.ds(pl.multiple_of(start, lane_cols), lane_cols)
+        src = terms.at[c, d, pl.ds(pl.multiple_of(group * rh, rh), rh), lanes(which)]
+        return pltpu.make_async_copy(src, out.at[:, span], own_s.at[key])
+
+    def peer_copy(c, d, which, key):
+        start = (2 * c + which) * 2 * group_cols + group * group_cols + d * lane_cols
+        span = pl.ds(pl.multiple_of(start, lane_cols), lane_cols)
+        src = terms.at[c, d, pl.ds(pl.multiple_of(peer * rh, rh), rh), lanes(which)]
+        return across(src, out.at[:, span], ys, yr, key)
+
+    def chip_keys(c, d):
+        return [(which, (2 * c + d) * 2 + which) for which in range(2)]
+
+    def make_term(t, d):
+        c = source_at(d, t, core) // 2
+        value = None
+        for g in range(2):
+            depth_rows = pl.ds(g * out_depth, out_depth)
+            term = jnp.dot(att[g], wo[c, d, depth_rows, :], preferred_element_type=F32).astype(BF16).astype(F32)
+            value = term if value is None else value + term
+        terms[c, d] = value.astype(BF16)
+        for which, key in chip_keys(c, d):
+            peer_copy(c, d, which, key).start()
+            out_copy(c, d, which, key).start()
+
+    att_copy(0, sooner).wait_recv()
+    att_copy(1, rest).wait_recv()
+
+    def project_out(t, carry):
+        third.partner_wait(t)
+        for j in range(chunks_out):
+            @pl.when((t >= lead) & (t < chips - 1))
+            def _():
+                third.advance(t, j)
+
+            if j < 2:
+                make_term(t, j)
+        return carry
+
+    lax.fori_loop(0, chips, project_out, 0)
+
+    first.drain()
+    second.drain()
+    third.drain()
+    for j in range(parts):
+        for d in range(2):
+            for t in range(reach[d]):
+                kv_copy(me, ks, kr, d, t, j, neighbours[d]).wait_send()
+                kv_copy(me, kps, kpr, d, t, j, partner).wait_send()
+        kv_copy(me, kps, kpr, 0, chips - 1, j, partner).wait_send()
+    for d in range(2):
+        swap(d).wait_send()
+    att_copy(0, sooner).wait_send()
+    att_copy(1, rest).wait_send()
+
+    def finish(c, carry):
+        for d in range(2):
+            for which, key in chip_keys(c, d):
+                peer_copy(c, d, which, key).wait_send()
+                out_copy(c, d, which, key).wait()
+                peer_copy(c, d, which, key).wait_recv()
+        return carry
+
+    lax.fori_loop(0, chips, finish, 0)
+
+
+def tables_of(n, rows):
+    freq = ROPE_BASE ** (-2.0 * np.arange(HEAD_DIM // 2, dtype=np.float64) / HEAD_DIM)
+    freq = np.concatenate([freq, freq])
+    near = np.arange(rows, dtype=np.float64)[:, None] * freq
+    far = (np.arange(n, dtype=np.float64) * rows)[:, None, None] * freq
+    return [f(a).astype(np.float32) for a in (near, far) for f in (np.cos, np.sin)]
+
+
+def pair_local(n, hidden, norm_gain, w_query, w_key, w_value, bias_query, bias_key, bias_value, w_out):
+    rows, width = hidden.shape
+    cols = w_query.shape[1]
+    heads = cols // HEAD_DIM
+    early = heads // 2 * HEAD_DIM
+    chips = n // 2
+    slices = 2 * n
+    half_depth = w_query.shape[0] // 2
+    group_cols = w_out.shape[1] // 2
+    wide, narrow, fine = 4, 2, 4
+    vectors = [v.reshape(1, -1) for v in (norm_gain, bias_query, bias_key, bias_value)]
+    any_spec = pl.BlockSpec(memory_space=pl.ANY)
+    vmem = pl.BlockSpec(memory_space=pltpu.VMEM)
+    dma = pltpu.SemaphoreType.DMA
+    return pl.pallas_call(
+        functools.partial(pair_kernel, n, wide, narrow, fine),
+        out_shape=jax.ShapeDtypeStruct((rows // 2, w_out.shape[1] * n), BF16),
+        in_specs=[pl.BlockSpec(memory_space=pltpu.HBM)] * 5 + [vmem] * 8,
+        out_specs=any_spec,
+        scratch_shapes=[
+            pltpu.VMEM((rows, width), BF16),
+            pltpu.VMEM((slices, half_depth, 2 * HEAD_DIM + early), BF16),
+            pltpu.VMEM((slices, half_depth, cols - early), BF16),
+            pltpu.VMEM((chips, 2, 2 * w_out.shape[0], group_cols), BF16),
+            pltpu.VMEM((rows, 2 * HEAD_DIM + early), F32),
+            pltpu.VMEM((rows, cols - early), F32),
+            pltpu.VMEM((chips, 2 * rows, 2 * HEAD_DIM), BF16),
+            pltpu.VMEM((heads, rows, HEAD_DIM), BF16),
+            pltpu.VMEM((heads, rows, 1), F32),
+            pltpu.VMEM((heads, rows, 1), F32),
+            pltpu.VMEM((heads, rows, HEAD_DIM), F32),
+            pltpu.VMEM((2, rows, cols), BF16),
+            pltpu.VMEM((chips, 2, rows, group_cols), BF16),
+            dma((11,)),
+            dma((2,)), dma((2,)), dma((2,)), dma((2,)),
+            dma((4 * chips,)), dma((4 * chips,)), dma((4 * chips,)),
+        ]
+        + [dma((2 * chips * wide,))] * 4
+        + [dma((2 * chips * narrow,))] * 4
+        + [dma((2 * chips * fine,))] * 4
+        + [dma((4 * chips,))] * 4,
+        compiler_params=pltpu.CompilerParams(
+            collective_id=0, has_side_effects=True, vmem_limit_bytes=VMEM_LIMIT
+        ),
+    )(hidden, w_query, w_key, w_value, w_out, *vectors, *tables_of(n, rows))
+
+
+def fits_pair(n, groups, rows, w_query, w_out):
+    chips = n // 2
+    return (
+        groups == 2
+        and chips % 4 == 0
+        and rows % 32 == 0
+        and w_query.shape[1] % (2 * HEAD_DIM) == 0
+        and w_query.shape[0] % 128 == 0
+        and w_out.shape[1] % 512 == 0
+    )
+
+
 def local(n, groups, hidden, norm_gain, w_query, w_key, w_value, bias_query, bias_key, bias_value, w_out):
     rows, width = hidden.shape
+    if fits_pair(n, groups, rows, w_query, w_out):
+        return pair_local(n, hidden, norm_gain, w_query, w_key, w_value, bias_query, bias_key, bias_value, w_out)
     cols = w_query.shape[1]
     heads = cols // HEAD_DIM
     wide = cols + 2 * HEAD_DIM
@@ -376,11 +873,7 @@
     half_depth = w_query.shape[0] // 2
     half_cols = w_out.shape[1] // 2
 
-    freq = ROPE_BASE ** (-2.0 * np.arange(HEAD_DIM // 2, dtype=np.float64) / HEAD_DIM)
-    freq = np.concatenate([freq, freq])
-    near = np.arange(rows, dtype=np.float64)[:, None] * freq
-    far = (np.arange(n, dtype=np.float64) * rows)[:, None, None] * freq
-    tables = [f(a).astype(np.float32) for a in (near, far) for f in (np.cos, np.sin)]
+    tables = tables_of(n, rows)
     vectors = [v.reshape(1, -1) for v in (norm_gain, bias_query, bias_key, bias_value)]
 
     any_spec = pl.BlockSpec(memory_space=pl.ANY)

time: 156 us -> 149 us (0.955); the launches traced: 153 us -> 148 us
  Pallas kernels: 148 us -> 137 us
  local copies, waits for them, and re-layouts: 5.9 us -> 11.2 us
    pallas_call x1, Pallas kernels: 148 us -> 137 us  [pair_local(): pl.pallas_call(functools.partial(pair_kernel, n, wide, narrow, fine), out...]
    unnamed x1 -> x21, local copies, waits for them, and re-layouts: 3.27 us -> 9.81 us
where the time goes in v1:
time: 149 us; the launch traced here: 148 us
  Pallas kernels  137 us (92%)
  local copies, waits for them, and re-layouts  11.2 us (8%)
    pallas_call x1, Pallas kernels, pair_local(): pl.pallas_call(functools.partial(pair_kernel, n, wide, narrow, fine), out...  137 us
    unnamed x21, local copies, waits for them, and re-layouts  9.81 us

profile of v1, /device:TPU:0, one launch (start us, length us, event | category | flops | bytes accessed | tf_op | source)
XLA Modules:
  0.0 148.1 jit_solution(12122499474777061018)
XLA Ops:
  0.0 0.7 reshape.13.bias_query
  0.7 0.7 reshape.12.gain
  1.4 0.0 copy-start
  1.4 1.0 copy-done
  2.5 0.0 copy-start.1
  2.5 1.0 copy-done.1
  3.5 0.0 copy-start.2
  3.5 0.9 copy-done.2
  4.4 0.0 copy-start.3
  4.4 0.9 copy-done.3
  5.3 0.0 copy-start.4
  5.3 0.9 copy-done.4
  6.2 0.0 copy-start.5
  6.2 0.9 copy-done.5
  7.1 0.0 copy-start.6
  7.1 0.7 copy-done.6
  7.8 0.0 copy-start.7
  7.8 0.7 copy-done.7
  8.5 0.0 copy-start.8
  8.5 0.7 copy-done.8
  9.2 0.0 copy-start.9
  9.2 0.7 copy-done.9
  9.8 136.9 %shard_map.127 = bf16[144,8192]{1,0:T(8,128)(2,1)S(1)} custom-call(bf16[288,8192]{1,0:T(8,128)(2,1)} %hidden.1, bf16[512,512]{1,0:T(8,128)(2,1)S(1)} %copy-done, bf16[512,128]{1,0:T(8,128)(2,1)S(1)} %copy-done.4, bf16[512,128]{1,0:T(8,128)(2,1)S(1)} %copy-done.5, bf16[512,512]{1,0:T(8,128)(2,1)S(1)} %copy-done.1, bf16[1,8192]{1,0:T(2,128)(2,1)S(1)} %reshape.12.gain, ...), custom_call_target="tpu_custom_call" | custom-call | tf_op jit(solution)/shard_map/pallas_call | solution.py:817
  146.7 1.4 copy.15
Async XLA Ops:
  1.4 1.0 copy-start
  2.5 1.0 copy-start.1
  3.5 0.9 copy-start.2
  4.4 0.9 copy-start.3
  5.3 0.9 copy-start.4
  6.2 0.9 copy-start.5
  7.1 0.7 copy-start.6
  7.8 0.7 copy-start.7
  8.5 0.7 copy-start.8
  9.2 0.7 copy-start.9

commit v2 on v1

--- a/solution.py
+++ b/solution.py
@@ -14,7 +14,9 @@
 MESH = pl.DeviceIdType.MESH
 F32 = jnp.float32
 BF16 = jnp.bfloat16
-VMEM_LIMIT = 48 * 1024 * 1024
+OPS = (1, 0, 0, 1, 1, 8)
+PIECES = (4, 2, 4, 2)
+VMEM_LIMIT = 64 * 1024 * 1024 - 4096 * 1024
 
 
 def kernel(
@@ -367,15 +369,20 @@
 
 def pair_kernel(
     n, chunks_wide, chunks_narrow, chunks_out,
-    hidden, w_query, w_key, w_value, w_out, gain, bias_query, bias_key, bias_value,
-    near_cos, near_sin, far_cos, far_sin,
-    out,
-    hid, w_first, w_second, wo, acc_first, acc_second, kv_all, q_ref, high, total, mixed, att, terms,
+    hidden, w_query, w_key, w_value, w_out, *rest_refs,
+):
+    small = rest_refs[:8]
+    out = rest_refs[8]
+    held = rest_refs[9:17]
+    gain, bias_query, bias_key, bias_value, near_cos, near_sin, far_cos, far_sin = held
+    (
+    gains, small_sem, hid, w_first, w_second, wo, acc_first, acc_second, kv_all, q_ref, high, total, mixed, att, terms,
     load_sem, swap_s, swap_r, att_s, att_r, own_s, ys, yr,
     fs, fr, fps, fpr, ss, sr, sps, spr, os_, or_, ops, opr, ks, kr, kps, kpr,
-):
+    ) = rest_refs[17:]
     chips = n // 2
     depth = chips // 2
+    ops_from, ops_first, ops_busy, ops_calm, ops_gap, ops_rest = OPS
     me = lax.axis_index("seq")
     group = lax.axis_index("head")
     peer = 1 - group
@@ -436,7 +443,8 @@
         last.append((w_out.at[:, wo_lanes(group, h)], wo.at[chip, h, group_rows(group), lanes(core)]))
     later.append((hidden, hid))
     copies = [pltpu.make_async_copy(a, b, load_sem.at[i]) for i, (a, b) in enumerate(loads + later + last)]
-    for copy in copies:
+    small_copies = [pltpu.make_async_copy(a, b, small_sem.at[i]) for i, (a, b) in enumerate(zip(small, held))]
+    for copy in copies[: len(loads)]:
         copy.start()
 
     barrier = pltpu.get_barrier_semaphore()
@@ -484,6 +492,16 @@
 
                 remote(block, psend, precv, self.key(d, t, j), partner).start()
 
+        def op(self, index):
+            @pl.when(index < self.pieces)
+            def _():
+                self.begin(index)
+
+            @pl.when((index >= self.pieces) & (index < self.pieces * chips))
+            def _():
+                done = index - self.pieces
+                self.advance(done // self.pieces, done % self.pieces)
+
         def partner_wait(self, t):
             send, recv, psend, precv = self.sems
             for j in range(self.pieces):
@@ -526,11 +544,18 @@
         first.begin(j)
     for d in range(2):
         swap(d).start()
+    for copy in copies[len(loads):] + small_copies:
+        copy.start()
     for copy in copies[len(loads):]:
         copy.wait()
 
+    for copy in small_copies:
+        copy.wait()
+    gains[...] = gain[...].astype(F32)
+
     slices = 2 * n
     step_cols = width // slices
+    gain_rows = step_cols // HEAD_DIM
 
     def columns(i):
         return pl.ds(pl.multiple_of(i * step_cols, step_cols), step_cols)
@@ -543,18 +568,22 @@
     inverse = lax.rsqrt(jnp.sum(squares, axis=-1, keepdims=True) * (1.0 / width) + EPSILON)
 
     def normed(i):
-        scaled = hid[:, columns(i)].astype(F32) * inverse * gain[:, columns(i)].astype(F32)
+        line = jnp.concatenate([gains[pl.ds(i * gain_rows + r, 1), :] for r in range(gain_rows)], axis=1)
+        scaled = hid[:, columns(i)].astype(F32) * inverse * line
         value = scaled.astype(BF16)
         hid[:, columns(i)] = value
         return value
 
-    def widen(value, size):
-        return jnp.broadcast_to(value.astype(F32), (rows, size))
-
-    acc_first[:, pl.ds(0, HEAD_DIM)] = widen(bias_key[...], HEAD_DIM)
-    acc_first[:, pl.ds(HEAD_DIM, HEAD_DIM)] = widen(bias_value[...], HEAD_DIM)
-    acc_first[:, pl.ds(2 * HEAD_DIM, q_early)] = widen(bias_query[:, pl.ds(0, q_early)], q_early)
-    acc_second[...] = widen(bias_query[:, pl.ds(q_early, q_late)], q_late)
+    def widen(line):
+        return jnp.broadcast_to(line.astype(F32), (rows, HEAD_DIM))
+
+    acc_first[:, pl.ds(0, HEAD_DIM)] = widen(bias_key[...])
+    acc_first[:, pl.ds(HEAD_DIM, HEAD_DIM)] = widen(bias_value[...])
+    lines = bias_query[...].astype(F32)
+    for h in range(early):
+        acc_first[:, pl.ds((2 + h) * HEAD_DIM, HEAD_DIM)] = widen(lines[h : h + 1])
+    for h in range(early, heads):
+        acc_second[:, pl.ds((h - early) * HEAD_DIM, HEAD_DIM)] = widen(lines[h : h + 1])
 
     def project_first(t, carry):
         @pl.when(t < chips - 1)
@@ -566,6 +595,20 @@
         def _():
             for j in range(chunks_narrow):
                 second.begin(j)
+
+        @pl.when(t == ops_from)
+        def _():
+            for d in range(2):
+                swap(d).wait_recv()
+
+        @pl.when((t >= ops_from) & (t < ops_from + ops_first))
+        def _():
+            third.op(t - ops_from)
+
+        @pl.when(t == chips - 1)
+        def _():
+            for j in range(chunks_narrow):
+                second.advance(0, j)
 
         first.partner_wait(t)
         for d in range(2):
@@ -596,7 +639,7 @@
         q_ref[h] = rotary(acc_first[:, pl.ds((2 + h) * HEAD_DIM, HEAD_DIM)]).astype(BF16)
 
     reach = (chips // 2, chips - 1 - chips // 2)
-    parts = 2 if rows % 32 == 0 else 1
+    parts = PIECES[3]
     piece_rows = rows // parts
 
     def kv_copy(owner, send, recv, direction, step, j, device):
@@ -608,8 +651,6 @@
         for d in range(2):
             kv_copy(me, ks, kr, d, 0, j, neighbours[d]).start()
         kv_copy(me, kps, kpr, 0, chips - 1, j, partner).start()
-    for j in range(chunks_narrow):
-        second.advance(0, j)
 
     factor = HEAD_DIM ** (-0.5) * 1.4426950408889634
 
@@ -645,9 +686,6 @@
         kv_copy(partner, kps, kpr, 0, chips - 1, j, partner).wait_recv()
     attend(chip, True, sooner)
 
-    for d in range(2):
-        swap(d).wait_recv()
-
     def attention(t, carry):
         for j in range(parts):
             for d in range(2):
@@ -667,10 +705,13 @@
             for j in range(chunks_narrow):
                 second.advance(t + 1, j)
 
-        for j in range(chunks_out):
-            @pl.when(t == min(reach[0] - 1 + j, chips - 3))
+        busy = reach[0] - 1
+        for k in range(max(ops_busy, ops_calm)):
+            index = ops_first + ops_busy * jnp.minimum(t, busy) + ops_calm * jnp.maximum(t - busy, 0) + k
+
+            @pl.when(((t < busy) & (k < ops_busy)) | ((t >= busy) & (k < ops_calm)))
             def _():
-                third.begin(j)
+                third.op(index)
 
         for d in range(2):
             @pl.when((t > 0) & (t <= reach[d]))
@@ -711,8 +752,13 @@
     att_copy(0, sooner).start()
     attend(chip, True, rest)
 
+    ops_middle = ops_first + ops_busy * (reach[0] - 1) + ops_calm * (chips + 1 - reach[0])
+    ops_done = ops_middle + ops_rest
+
     def attention_rest(c, carry):
-        third.advance(c // chunks_out, c % chunks_out)
+        @pl.when((c % ops_gap == 0) & (c // ops_gap < ops_rest))
+        def _():
+            third.op(ops_middle + c // ops_gap)
 
         @pl.when(c < chip)
         def _():
@@ -722,7 +768,6 @@
     lax.fori_loop(0, chips, attention_rest, 0)
     settle(rest)
     att_copy(1, rest).start()
-    lead = chips // chunks_out
 
     def out_copy(c, d, which, key):
         start = (2 * c + which) * 2 * group_cols + group * group_cols + d * lane_cols
@@ -757,7 +802,7 @@
     def project_out(t, carry):
         third.partner_wait(t)
         for j in range(chunks_out):
-            @pl.when((t >= lead) & (t < chips - 1))
+            @pl.when(((t + 1) * chunks_out + j >= ops_done) & (t < chips - 1))
             def _():
                 third.advance(t, j)
 
@@ -809,17 +854,21 @@
     slices = 2 * n
     half_depth = w_query.shape[0] // 2
     group_cols = w_out.shape[1] // 2
-    wide, narrow, fine = 4, 2, 4
-    vectors = [v.reshape(1, -1) for v in (norm_gain, bias_query, bias_key, bias_value)]
+    wide, narrow, fine, parts = PIECES
+    vectors = [v.reshape(-1, HEAD_DIM) for v in (norm_gain, bias_query, bias_key, bias_value)]
+    small = vectors + tables_of(n, rows)
+    result = jax.ShapeDtypeStruct((rows // 2, w_out.shape[1] * n), BF16)
     any_spec = pl.BlockSpec(memory_space=pl.ANY)
-    vmem = pl.BlockSpec(memory_space=pltpu.VMEM)
     dma = pltpu.SemaphoreType.DMA
     return pl.pallas_call(
         functools.partial(pair_kernel, n, wide, narrow, fine),
-        out_shape=jax.ShapeDtypeStruct((rows // 2, w_out.shape[1] * n), BF16),
-        in_specs=[pl.BlockSpec(memory_space=pltpu.HBM)] * 5 + [vmem] * 8,
-        out_specs=any_spec,
-        scratch_shapes=[
+        out_shape=pltpu.VMEM(result.shape, result.dtype),
+        in_specs=[any_spec] * 13,
+        out_specs=pl.BlockSpec(memory_space=pltpu.VMEM),
+        scratch_shapes=[pltpu.VMEM(a.shape, a.dtype) for a in small]
+        + [
+            pltpu.VMEM((width // HEAD_DIM, HEAD_DIM), F32),
+            dma((8,)),
             pltpu.VMEM((rows, width), BF16),
             pltpu.VMEM((slices, half_depth, 2 * HEAD_DIM + early), BF16),
             pltpu.VMEM((slices, half_depth, cols - early), BF16),
@@ -842,9 +891,9 @@
         + [dma((2 * chips * fine,))] * 4
         + [dma((4 * chips,))] * 4,
         compiler_params=pltpu.CompilerParams(
-            collective_id=0, has_side_effects=True, vmem_limit_bytes=VMEM_LIMIT
+            collective_id=0, has_side_effects=True, vmem_limit_bytes=VMEM_LIMIT - 2 * result.size
         ),
-    )(hidden, w_query, w_key, w_value, w_out, *vectors, *tables_of(n, rows))
+    )(hidden, w_query, w_key, w_value, w_out, *small)
 
 
 def fits_pair(n, groups, rows, w_query, w_out):

time: 149 us -> 137 us (0.919)
  local copies, waits for them, and re-layouts: 11.2 us -> 1.41 us
  Pallas kernels: 137 us -> 135 us
    unnamed x21 -> x1, local copies, waits for them, and re-layouts: 9.81 us -> 1.41 us
    pallas_call x1, Pallas kernels: 137 us -> 135 us  [pair_local(): pl.pallas_call(functools.partial(pair_kernel, n, wide, narrow, fine), out...]
where the time goes in v2:
time: 137 us; the launch traced here: 136 us
  Pallas kernels  135 us (99%)
  local copies, waits for them, and re-layouts  1.41 us (1%)
    pallas_call x1, Pallas kernels, pair_local(): pl.pallas_call(functools.partial(pair_kernel, n, wide, narrow, fine), out...  135 us

profile of v2, /device:TPU:0, one launch (start us, length us, event | category | flops | bytes accessed | tf_op | source)
XLA Modules:
  0.0 136.4 jit_solution(11387993170797488674)
XLA Ops:
  0.0 135.0 %shard_map.127 = bf16[144,8192]{1,0:T(8,128)(2,1)S(1)} custom-call(bf16[288,8192]{1,0:T(8,128)(2,1)} %hidden.1, bf16[512,512]{1,0:T(8,128)(2,1)} %w_query.1, bf16[512,128]{1,0:T(8,128)(2,1)} %w_key.1, bf16[512,128]{1,0:T(8,128)(2,1)} %w_value.1, bf16[512,512]{1,0:T(8,128)(2,1)} %w_out.1, bf16[64,128]{1,0:T(8,128)(2,1)} %bitcast.4, bf16[4,128]{1,0:T(4,128)(2,1)} %bitcast.5, ...), custom_call_target="tpu_custom_call" | custom-call | tf_op jit(solution)/shard_map/pallas_call | solution.py:863
  135.0 1.4 %copy.15 = bf16[144,8192]{1,0:T(8,128)(2,1)} copy(bf16[144,8192]{1,0:T(8,128)(2,1)S(1)} %shard_map.127) | data formatting | bytes 4718592

commit v3 on v2

--- a/solution.py
+++ b/solution.py
@@ -14,8 +14,9 @@
 MESH = pl.DeviceIdType.MESH
 F32 = jnp.float32
 BF16 = jnp.bfloat16
-OPS = (1, 0, 0, 1, 1, 8)
-PIECES = (4, 2, 4, 2)
+OPS = (6, 1, 0, 1)
+PIECES = (2, 2, 2)
+STACK = 2
 VMEM_LIMIT = 64 * 1024 * 1024 - 4096 * 1024
 
 
@@ -368,7 +369,7 @@
 
 
 def pair_kernel(
-    n, chunks_wide, chunks_narrow, chunks_out,
+    n, chunks_in, chunks_out, parts,
     hidden, w_query, w_key, w_value, w_out, *rest_refs,
 ):
     small = rest_refs[:8]
@@ -376,13 +377,14 @@
     held = rest_refs[9:17]
     gain, bias_query, bias_key, bias_value, near_cos, near_sin, far_cos, far_sin = held
     (
-    gains, small_sem, hid, w_first, w_second, wo, acc_first, acc_second, kv_all, q_ref, high, total, mixed, att, terms,
-    load_sem, swap_s, swap_r, att_s, att_r, own_s, ys, yr,
-    fs, fr, fps, fpr, ss, sr, sps, spr, os_, or_, ops, opr, ks, kr, kps, kpr,
+    gains, small_sem, hid, w_all, wo, acc, kv_all, q_ref, high, total, mixed, att, terms, wo_own,
+    own_s, own_r, load_sem, swap_s, swap_r, att_s, att_r, ys, yr,
+    ws, wr, wps, wpr, os_, or_, ops, opr, ks, kr, kps, kpr,
     ) = rest_refs[17:]
     chips = n // 2
     depth = chips // 2
-    ops_from, ops_first, ops_busy, ops_calm, ops_gap, ops_rest = OPS
+    ops_from, ops_first, ops_busy, ops_calm = OPS
+    stack = STACK
     me = lax.axis_index("seq")
     group = lax.axis_index("head")
     peer = 1 - group
@@ -408,9 +410,6 @@
     half_depth = w_query.shape[0] // 2
     q_cols = w_query.shape[1]
     heads = q_cols // HEAD_DIM
-    early = heads // 2
-    q_early = early * HEAD_DIM
-    q_late = q_cols - q_early
     out_depth = w_out.shape[0]
     group_cols = w_out.shape[1] // 2
     lane_cols = group_cols // 2
@@ -432,17 +431,16 @@
     def group_rows(which):
         return pl.ds(pl.multiple_of(which * out_depth, out_depth), out_depth)
 
-    loads, later, last = [], [], []
+    loads, last = [], []
     for h in range(2):
         span = pl.ds(h * half_depth, half_depth)
-        slot = w_first.at[2 * me + h]
+        slot = w_all.at[2 * me + h]
         loads.append((w_key.at[span], slot.at[:, pl.ds(0, HEAD_DIM)]))
         loads.append((w_value.at[span], slot.at[:, pl.ds(HEAD_DIM, HEAD_DIM)]))
-        loads.append((w_query.at[span, pl.ds(0, q_early)], slot.at[:, pl.ds(2 * HEAD_DIM, q_early)]))
-        later.append((w_query.at[span, pl.ds(q_early, q_late)], w_second.at[2 * me + h]))
+        loads.append((w_query.at[span], slot.at[:, pl.ds(2 * HEAD_DIM, q_cols)]))
         last.append((w_out.at[:, wo_lanes(group, h)], wo.at[chip, h, group_rows(group), lanes(core)]))
-    later.append((hidden, hid))
-    copies = [pltpu.make_async_copy(a, b, load_sem.at[i]) for i, (a, b) in enumerate(loads + later + last)]
+        last.append((w_out.at[:, wo_lanes(peer, h)], wo_own.at[h, group_rows(group), lanes(core)]))
+    copies = [pltpu.make_async_copy(a, b, load_sem.at[i]) for i, (a, b) in enumerate(loads + [(hidden, hid)] + last)]
     small_copies = [pltpu.make_async_copy(a, b, small_sem.at[i]) for i, (a, b) in enumerate(zip(small, held))]
     for copy in copies[: len(loads)]:
         copy.start()
@@ -464,6 +462,14 @@
             w_out.at[:, wo_lanes(peer, d)], wo.at[chip, d, group_rows(group), lanes(core)], swap_s, swap_r, d
         )
 
+    def swap_own(d):
+        return across(
+            w_out.at[:, wo_lanes(group, d)], wo_own.at[d, group_rows(group), lanes(core)], swap_s, swap_r, 2 + d
+        )
+
+    def own_copy(d, which):
+        return remote(wo_own.at[d, :, lanes(which)], own_s, own_r, d, partner)
+
     class Ring:
         def __init__(self, view, sems, pieces):
             self.view, self.sems, self.pieces = view, sems, pieces
@@ -502,9 +508,9 @@
                 done = index - self.pieces
                 self.advance(done // self.pieces, done % self.pieces)
 
-        def partner_wait(self, t):
+        def partner_wait(self, t, some=None):
             send, recv, psend, precv = self.sems
-            for j in range(self.pieces):
+            for j in range(self.pieces) if some is None else some:
                 for d in range(2):
                     block = self.view(source_at(d, t, 1 - core), d, j)
                     remote(block, psend, precv, self.key(d, (t + chips - 1) % chips, j), partner).wait_recv()
@@ -534,16 +540,17 @@
         size = wo.shape[2] // chunks_out
         return wo.at[owner // 2, d, pl.ds(pl.multiple_of(j * size, size), size), lanes(owner % 2)]
 
-    first = Ring(rows_view(w_first, chunks_wide), (fs, fr, fps, fpr), chunks_wide)
-    second = Ring(rows_view(w_second, chunks_narrow), (ss, sr, sps, spr), chunks_narrow)
+    first = Ring(rows_view(w_all, chunks_in), (ws, wr, wps, wpr), chunks_in)
     third = Ring(wo_view, (os_, or_, ops, opr), chunks_out)
 
     for copy in copies[: len(loads)]:
         copy.wait()
-    for j in range(chunks_wide):
+    for j in range(chunks_in):
         first.begin(j)
     for d in range(2):
         swap(d).start()
+    for d in range(2):
+        swap_own(d).start()
     for copy in copies[len(loads):] + small_copies:
         copy.start()
     for copy in copies[len(loads):]:
@@ -570,56 +577,48 @@
     def normed(i):
         line = jnp.concatenate([gains[pl.ds(i * gain_rows + r, 1), :] for r in range(gain_rows)], axis=1)
         scaled = hid[:, columns(i)].astype(F32) * inverse * line
-        value = scaled.astype(BF16)
-        hid[:, columns(i)] = value
-        return value
+        return scaled.astype(BF16)
 
     def widen(line):
         return jnp.broadcast_to(line.astype(F32), (rows, HEAD_DIM))
 
-    acc_first[:, pl.ds(0, HEAD_DIM)] = widen(bias_key[...])
-    acc_first[:, pl.ds(HEAD_DIM, HEAD_DIM)] = widen(bias_value[...])
+    acc[:, pl.ds(0, HEAD_DIM)] = widen(bias_key[...])
+    acc[:, pl.ds(HEAD_DIM, HEAD_DIM)] = widen(bias_value[...])
     lines = bias_query[...].astype(F32)
-    for h in range(early):
-        acc_first[:, pl.ds((2 + h) * HEAD_DIM, HEAD_DIM)] = widen(lines[h : h + 1])
-    for h in range(early, heads):
-        acc_second[:, pl.ds((h - early) * HEAD_DIM, HEAD_DIM)] = widen(lines[h : h + 1])
-
-    def project_first(t, carry):
+    for h in range(heads):
+        acc[:, pl.ds((2 + h) * HEAD_DIM, HEAD_DIM)] = widen(lines[h : h + 1])
+
+    def project(t, carry):
         @pl.when(t < chips - 1)
         def _():
-            for j in range(chunks_wide):
+            for j in range(chunks_in):
                 first.advance(t, j)
 
-        @pl.when(t == chips - 3)
-        def _():
-            for j in range(chunks_narrow):
-                second.begin(j)
-
         @pl.when(t == ops_from)
         def _():
             for d in range(2):
                 swap(d).wait_recv()
 
+        @pl.when(t == chips // 2)
+        def _():
+            for d in range(2):
+                swap_own(d).wait_recv()
+                own_copy(d, core).start()
+
         @pl.when((t >= ops_from) & (t < ops_from + ops_first))
         def _():
             third.op(t - ops_from)
-
-        @pl.when(t == chips - 1)
-        def _():
-            for j in range(chunks_narrow):
-                second.advance(0, j)
 
         first.partner_wait(t)
         for d in range(2):
             i = 2 * source_at(d, t, core) + d
             k = 2 * source_at(d, t, 1 - core) + d
-            acc_first[...] += jnp.dot(normed(i), w_first[i], preferred_element_type=F32) + jnp.dot(
-                normed(k), w_first[k], preferred_element_type=F32
+            acc[...] += jnp.dot(normed(i), w_all[i], preferred_element_type=F32) + jnp.dot(
+                normed(k), w_all[k], preferred_element_type=F32
             )
         return carry
 
-    lax.fori_loop(0, chips, project_first, 0)
+    lax.fori_loop(0, chips, project, 0)
 
     block_cos, block_sin = far_cos[me], far_sin[me]
     cosine = near_cos[...] * block_cos - near_sin[...] * block_sin
@@ -633,13 +632,12 @@
     def kv_rows(which):
         return pl.ds(pl.multiple_of(which * rows, rows), rows)
 
-    kv_all[chip, kv_rows(core), pl.ds(0, HEAD_DIM)] = rotary(acc_first[:, pl.ds(0, HEAD_DIM)]).astype(BF16)
-    kv_all[chip, kv_rows(core), pl.ds(HEAD_DIM, HEAD_DIM)] = acc_first[:, pl.ds(HEAD_DIM, HEAD_DIM)].astype(BF16)
-    for h in range(early):
-        q_ref[h] = rotary(acc_first[:, pl.ds((2 + h) * HEAD_DIM, HEAD_DIM)]).astype(BF16)
-
-    reach = (chips // 2, chips - 1 - chips // 2)
-    parts = PIECES[3]
+    kv_all[chip, kv_rows(core), pl.ds(0, HEAD_DIM)] = rotary(acc[:, pl.ds(0, HEAD_DIM)]).astype(BF16)
+    kv_all[chip, kv_rows(core), pl.ds(HEAD_DIM, HEAD_DIM)] = acc[:, pl.ds(HEAD_DIM, HEAD_DIM)].astype(BF16)
+    q_ref[pl.ds(0, rows), :] = rotary(acc[:, pl.ds(2 * HEAD_DIM, HEAD_DIM)]).astype(BF16)
+
+    far_steps = chips // 2
+    reach = [[far_steps - (j * 2 // parts != d) for j in range(parts)] for d in range(2)]
     piece_rows = rows // parts
 
     def kv_copy(owner, send, recv, direction, step, j, device):
@@ -651,22 +649,25 @@
         for d in range(2):
             kv_copy(me, ks, kr, d, 0, j, neighbours[d]).start()
         kv_copy(me, kps, kpr, 0, chips - 1, j, partner).start()
+    for h in range(1, heads):
+        q_ref[pl.ds(h * rows, rows), :] = rotary(acc[:, pl.ds((2 + h) * HEAD_DIM, HEAD_DIM)]).astype(BF16)
 
     factor = HEAD_DIM ** (-0.5) * 1.4426950408889634
 
-    def attend(c, own, which):
-        for h in which:
+    def attend(c, own):
+        for h in range(0, heads, stack):
+            some = pl.ds(h * rows, stack * rows)
             scores = lax.dot_general(
-                q_ref[h], kv_all[c, :, pl.ds(0, HEAD_DIM)], (((1,), (1,)), ((), ())),
+                q_ref[some, :], kv_all[c, :, pl.ds(0, HEAD_DIM)], (((1,), (1,)), ((), ())),
                 preferred_element_type=F32,
             )
             if own:
-                row = lax.broadcasted_iota(jnp.int32, scores.shape, 0) + core * rows
+                row = lax.broadcasted_iota(jnp.int32, scores.shape, 0) % rows + core * rows
                 col = lax.broadcasted_iota(jnp.int32, scores.shape, 1)
                 scores = jnp.where(row >= col, scores, -jnp.inf)
             top = jnp.max(scores, axis=-1, keepdims=True)
             if not own:
-                old = high[h]
+                old = high[some, :]
                 top = jnp.maximum(old, top)
             probs = jnp.exp2((scores - top) * factor)
             part = jnp.sum(probs, axis=-1, keepdims=True)
@@ -675,163 +676,182 @@
             )
             if not own:
                 shrink = jnp.exp2((old - top) * factor)
-                part = part + total[h] * shrink
-                product = product + mixed[h] * shrink
-            high[h] = top
-            total[h] = part
-            mixed[h] = product
-
-    sooner, rest = range(early), range(early, heads)
+                part = part + total[some, :] * shrink
+                product = product + mixed[some, :] * shrink
+            high[some, :] = top
+            total[some, :] = part
+            mixed[some, :] = product
+
     for j in range(parts):
         kv_copy(partner, kps, kpr, 0, chips - 1, j, partner).wait_recv()
-    attend(chip, True, sooner)
+    attend(chip, True)
+
+    busy_steps = far_steps - 1
 
     def attention(t, carry):
         for j in range(parts):
             for d in range(2):
-                @pl.when(t < reach[d])
+                @pl.when(t < reach[d][j])
                 def _():
                     owner = source_at(d, t + 1, core)
                     kv_copy(owner, ks, kr, d, t, j, neighbours[d]).wait_recv()
 
-                    @pl.when(t + 1 < reach[d])
+                    @pl.when(t + 1 < reach[d][j])
                     def _():
                         kv_copy(owner, ks, kr, d, t + 1, j, neighbours[d]).start()
 
                     kv_copy(owner, kps, kpr, d, t, j, partner).start()
 
-        @pl.when(t + 1 < chips - 1)
-        def _():
-            for j in range(chunks_narrow):
-                second.advance(t + 1, j)
-
-        busy = reach[0] - 1
         for k in range(max(ops_busy, ops_calm)):
-            index = ops_first + ops_busy * jnp.minimum(t, busy) + ops_calm * jnp.maximum(t - busy, 0) + k
-
-            @pl.when(((t < busy) & (k < ops_busy)) | ((t >= busy) & (k < ops_calm)))
+            index = ops_first + ops_busy * jnp.minimum(t, busy_steps) + ops_calm * jnp.maximum(t - busy_steps, 0) + k
+
+            @pl.when(((t < busy_steps) & (k < ops_busy)) | ((t >= busy_steps) & (k < ops_calm)))
             def _():
                 third.op(index)
 
-        for d in range(2):
-            @pl.when((t > 0) & (t <= reach[d]))
+        for j in range(parts):
+            for d in range(2):
+                @pl.when((t > 0) & (t <= reach[d][j]))
+                def _():
+                    owner = source_at(d, t, 1 - core)
+                    kv_copy(owner, kps, kpr, d, t - 1, j, partner).wait_recv()
+
+        for d in range(2):
+            other = source_at(d, t, core) // 2
+
+            @pl.when((t > 0) & (t <= far_steps - d) & (other < chip))
             def _():
-                owner = source_at(d, t, 1 - core)
-                for j in range(parts):
-                    kv_copy(owner, kps, kpr, d, t - 1, j, partner).wait_recv()
-
-                @pl.when(owner // 2 < chip)
-                def _():
-                    attend(owner // 2, False, sooner)
-
-        second.partner_wait(t)
-        for d in range(2):
-            i = 2 * source_at(d, t, core) + d
-            k = 2 * source_at(d, t, 1 - core) + d
-            acc_second[...] += jnp.dot(hid[:, columns(i)], w_second[i], preferred_element_type=F32) + jnp.dot(
-                hid[:, columns(k)], w_second[k], preferred_element_type=F32
-            )
+                attend(other, False)
         return carry
 
-    lax.fori_loop(0, chips, attention, 0)
-
-    def head_span(which):
-        return pl.ds(which[0] * HEAD_DIM, len(which) * HEAD_DIM)
-
-    def att_copy(key, which):
-        ref = att.at[group, :, head_span(which)]
+    lax.fori_loop(0, far_steps + 1, attention, 0)
+    ops_done = ops_first + ops_busy * busy_steps + ops_calm * (far_steps + 1 - busy_steps)
+
+    def row_span(which):
+        return pl.ds(pl.multiple_of(which * rh, rh), rh)
+
+    def att_copy(key):
+        ref = att.at[group, row_span((group + key) % 2), :]
         return across(ref, ref, att_s, att_r, key)
 
-    def settle(which):
-        for h in which:
-            att[group, :, pl.ds(h * HEAD_DIM, HEAD_DIM)] = (mixed[h] / total[h]).astype(BF16)
-
-    settle(sooner)
-    for h in rest:
-        q_ref[h] = rotary(acc_second[:, pl.ds((h - early) * HEAD_DIM, HEAD_DIM)]).astype(BF16)
-    att_copy(0, sooner).start()
-    attend(chip, True, rest)
-
-    ops_middle = ops_first + ops_busy * (reach[0] - 1) + ops_calm * (chips + 1 - reach[0])
-    ops_done = ops_middle + ops_rest
-
-    def attention_rest(c, carry):
-        @pl.when((c % ops_gap == 0) & (c // ops_gap < ops_rest))
-        def _():
-            third.op(ops_middle + c // ops_gap)
-
-        @pl.when(c < chip)
-        def _():
-            attend(c, False, rest)
-        return carry
-
-    lax.fori_loop(0, chips, attention_rest, 0)
-    settle(rest)
-    att_copy(1, rest).start()
-
-    def out_copy(c, d, which, key):
+    for h in range(heads):
+        att[group, :, pl.ds(h * HEAD_DIM, HEAD_DIM)] = (
+            mixed[pl.ds(h * rows, rows), :] / total[pl.ds(h * rows, rows), :]
+        ).astype(BF16)
+    for key in range(2):
+        att_copy(key).start()
+
+    def out_span(c, d, which):
         start = (2 * c + which) * 2 * group_cols + group * group_cols + d * lane_cols
-        span = pl.ds(pl.multiple_of(start, lane_cols), lane_cols)
-        src = terms.at[c, d, pl.ds(pl.multiple_of(group * rh, rh), rh), lanes(which)]
-        return pltpu.make_async_copy(src, out.at[:, span], own_s.at[key])
-
-    def peer_copy(c, d, which, key):
-        start = (2 * c + which) * 2 * group_cols + group * group_cols + d * lane_cols
-        span = pl.ds(pl.multiple_of(start, lane_cols), lane_cols)
-        src = terms.at[c, d, pl.ds(pl.multiple_of(peer * rh, rh), rh), lanes(which)]
-        return across(src, out.at[:, span], ys, yr, key)
-
-    def chip_keys(c, d):
-        return [(which, (2 * c + d) * 2 + which) for which in range(2)]
-
-    def make_term(t, d):
+        return pl.ds(pl.multiple_of(start, lane_cols), lane_cols)
+
+    def term_copy(c, d, which):
+        src = terms.at[c, d, :, pl.ds(which * lane_cols, lane_cols)]
+        return across(src, out.at[:, out_span(c, d, which)], ys, yr, (2 * c + d) * 2 + which)
+
+    def part(weights, which, g):
+        return jnp.dot(
+            att[g, row_span(which), :], weights[pl.ds(g * out_depth, out_depth), :], preferred_element_type=F32
+        ).astype(BF16).astype(F32)
+
+    def product(weights, which):
+        return (part(weights, which, 0) + part(weights, which, 1)).astype(BF16)
+
+    def send_terms(c, d, value):
+        terms[c, d] = value
+        for which in range(2):
+            term_copy(c, d, which).start()
+
+    def give(t, d):
         c = source_at(d, t, core) // 2
-        value = None
-        for g in range(2):
-            depth_rows = pl.ds(g * out_depth, out_depth)
-            term = jnp.dot(att[g], wo[c, d, depth_rows, :], preferred_element_type=F32).astype(BF16).astype(F32)
-            value = term if value is None else value + term
-        terms[c, d] = value.astype(BF16)
-        for which, key in chip_keys(c, d):
-            peer_copy(c, d, which, key).start()
-            out_copy(c, d, which, key).start()
-
-    att_copy(0, sooner).wait_recv()
-    att_copy(1, rest).wait_recv()
+        send_terms(c, d, product(wo.at[c, d], peer))
+
+    def put(c, d, owner, value):
+        for which in range(2):
+            start = (2 * c + which) * 2 * group_cols + owner * group_cols + d * lane_cols
+            span = pl.ds(pl.multiple_of(start, lane_cols), lane_cols)
+            out[:, span] = value[:, which * lane_cols : (which + 1) * lane_cols]
+
+    def keep(t, d):
+        c = source_at(d, t, core) // 2
+        put(c, d, group, product(wo.at[c, d], group))
+
+    def keep_own(d):
+        put(chip, d, group, product(wo.at[chip, d], group))
+        put(chip, d, peer, product(wo_own.at[d], group))
+
+    third.partner_wait(0)
 
     def project_out(t, carry):
         third.partner_wait(t)
-        for j in range(chunks_out):
-            @pl.when(((t + 1) * chunks_out + j >= ops_done) & (t < chips - 1))
+
+        @pl.when(t == 1)
+        def _():
+            att_copy(0).wait_recv()
+
+        def move(j):
+            @pl.when((t + 1) * chunks_out + j >= ops_done)
             def _():
                 third.advance(t, j)
 
-            if j < 2:
-                make_term(t, j)
+        for j in range(chunks_out - 1):
+            move(j)
+        for d in range(2):
+            give(t, d)
+
+        @pl.when(t == 1)
+        def _():
+            att_copy(1).wait_recv()
+
+        for d in range(2):
+            keep(t, d)
+        move(chunks_out - 1)
+
+        @pl.when(t == chips // 2)
+        def _():
+            for d in range(2):
+                own_copy(d, 1 - core).wait_recv()
+                keep_own(d)
         return carry
 
-    lax.fori_loop(0, chips, project_out, 0)
+    for j in range(chunks_out):
+        if chunks_out + j >= ops_done:
+            third.advance(0, j)
+    lax.fori_loop(1, chips - 1, project_out, 0)
+    final = chips - 1
+    held_parts = []
+    for j in range(chunks_out):
+        third.partner_wait(final, (j,))
+        for d in range(2):
+            held_parts.append(part(wo.at[source_at(d, final, core) // 2, d], peer, j))
+    for d in range(2):
+        send_terms(source_at(d, final, core) // 2, d, (held_parts[d] + held_parts[2 + d]).astype(BF16))
+    for d in range(2):
+        keep(final, d)
+
 
     first.drain()
-    second.drain()
     third.drain()
     for j in range(parts):
         for d in range(2):
-            for t in range(reach[d]):
+            for t in range(reach[d][j]):
                 kv_copy(me, ks, kr, d, t, j, neighbours[d]).wait_send()
                 kv_copy(me, kps, kpr, d, t, j, partner).wait_send()
         kv_copy(me, kps, kpr, 0, chips - 1, j, partner).wait_send()
     for d in range(2):
         swap(d).wait_send()
-    att_copy(0, sooner).wait_send()
-    att_copy(1, rest).wait_send()
+        swap_own(d).wait_send()
+        own_copy(d, core).wait_send()
+    for key in range(2):
+        att_copy(key).wait_send()
 
     def finish(c, carry):
-        for d in range(2):
-            for which, key in chip_keys(c, d):
-                peer_copy(c, d, which, key).wait_send()
-                out_copy(c, d, which, key).wait()
-                peer_copy(c, d, which, key).wait_recv()
+        @pl.when(c != chip)
+        def _():
+            for d in range(2):
+                for which in range(2):
+                    term_copy(c, d, which).wait_send()
+                    term_copy(c, d, which).wait_recv()
         return carry
 
     lax.fori_loop(0, chips, finish, 0)
@@ -849,19 +869,18 @@
     rows, width = hidden.shape
     cols = w_query.shape[1]
     heads = cols // HEAD_DIM
-    early = heads // 2 * HEAD_DIM
     chips = n // 2
     slices = 2 * n
     half_depth = w_query.shape[0] // 2
     group_cols = w_out.shape[1] // 2
-    wide, narrow, fine, parts = PIECES
+    chunks_in, chunks_out, parts = PIECES
     vectors = [v.reshape(-1, HEAD_DIM) for v in (norm_gain, bias_query, bias_key, bias_value)]
     small = vectors + tables_of(n, rows)
     result = jax.ShapeDtypeStruct((rows // 2, w_out.shape[1] * n), BF16)
     any_spec = pl.BlockSpec(memory_space=pl.ANY)
     dma = pltpu.SemaphoreType.DMA
     return pl.pallas_call(
-        functools.partial(pair_kernel, n, wide, narrow, fine),
+        functools.partial(pair_kernel, n, chunks_in, chunks_out, parts),
         out_shape=pltpu.VMEM(result.shape, result.dtype),
         in_specs=[any_spec] * 13,
         out_specs=pl.BlockSpec(memory_space=pltpu.VMEM),
@@ -870,26 +889,25 @@
             pltpu.VMEM((width // HEAD_DIM, HEAD_DIM), F32),
             dma((8,)),
             pltpu.VMEM((rows, width), BF16),
-            pltpu.VMEM((slices, half_depth, 2 * HEAD_DIM + early), BF16),
-            pltpu.VMEM((slices, half_depth, cols - early), BF16),
+            pltpu.VMEM((slices, half_depth, 2 * HEAD_DIM + cols), BF16),
             pltpu.VMEM((chips, 2, 2 * w_out.shape[0], group_cols), BF16),
-            pltpu.VMEM((rows, 2 * HEAD_DIM + early), F32),
-            pltpu.VMEM((rows, cols - early), F32),
+            pltpu.VMEM((rows, 2 * HEAD_DIM + cols), F32),
             pltpu.VMEM((chips, 2 * rows, 2 * HEAD_DIM), BF16),
-            pltpu.VMEM((heads, rows, HEAD_DIM), BF16),
-            pltpu.VMEM((heads, rows, 1), F32),
-            pltpu.VMEM((heads, rows, 1), F32),
-            pltpu.VMEM((heads, rows, HEAD_DIM), F32),
+            pltpu.VMEM((heads * rows, HEAD_DIM), BF16),
+            pltpu.VMEM((heads * rows, 1), F32),
+            pltpu.VMEM((heads * rows, 1), F32),
+            pltpu.VMEM((heads * rows, HEAD_DIM), F32),
             pltpu.VMEM((2, rows, cols), BF16),
-            pltpu.VMEM((chips, 2, rows, group_cols), BF16),
+            pltpu.VMEM((chips, 2, rows // 2, group_cols), BF16),
+            pltpu.VMEM((2, 2 * w_out.shape[0], group_cols), BF16),
+            dma((2,)), dma((2,)),
             dma((11,)),
-            dma((2,)), dma((2,)), dma((2,)), dma((2,)),
-            dma((4 * chips,)), dma((4 * chips,)), dma((4 * chips,)),
+            dma((4,)), dma((4,)), dma((2,)), dma((2,)),
+            dma((4 * chips,)), dma((4 * chips,)),
         ]
-        + [dma((2 * chips * wide,))] * 4
-        + [dma((2 * chips * narrow,))] * 4
-        + [dma((2 * chips * fine,))] * 4
-        + [dma((4 * chips,))] * 4,
+        + [dma((2 * chips * chunks_in,))] * 4
+        + [dma((2 * chips * chunks_out,))] * 4
+        + [dma((2 * chips * parts,))] * 4,
         compiler_params=pltpu.CompilerParams(
             collective_id=0, has_side_effects=True, vmem_limit_bytes=VMEM_LIMIT - 2 * result.size
         ),
@@ -902,7 +920,7 @@
         groups == 2
         and chips % 4 == 0
         and rows % 32 == 0
-        and w_query.shape[1] % (2 * HEAD_DIM) == 0
+        and w_query.shape[1] % HEAD_DIM == 0
         and w_query.shape[0] % 128 == 0
         and w_out.shape[1] % 512 == 0
     )

time: 137 us -> 136 us (level)
  no operation moved by 1% of the time
where the time goes in v3:
time: 136 us
  Pallas kernels  134 us (99%)
  local copies, waits for them, and re-layouts  1.41 us (1%)
    pallas_call x1, Pallas kernels, pair_local(): pl.pallas_call(functools.partial(pair_kernel, n, chunks_in, chunks_out, p...  134 us

profile of v3, /device:TPU:0, one launch (start us, length us, event | category | flops | bytes accessed | tf_op | source)
XLA Modules:
  0.0 135.5 jit_solution(18342036206899335959)
XLA Ops:
  0.0 134.1 %shard_map.127 = bf16[144,8192]{1,0:T(8,128)(2,1)S(1)} custom-call(bf16[288,8192]{1,0:T(8,128)(2,1)} %hidden.1, bf16[512,512]{1,0:T(8,128)(2,1)} %w_query.1, bf16[512,128]{1,0:T(8,128)(2,1)} %w_key.1, bf16[512,128]{1,0:T(8,128)(2,1)} %w_value.1, bf16[512,512]{1,0:T(8,128)(2,1)} %w_out.1, bf16[64,128]{1,0:T(8,128)(2,1)} %bitcast.4, bf16[4,128]{1,0:T(4,128)(2,1)} %bitcast.5, ...), custom_call_target="tpu_custom_call" | custom-call | tf_op jit(solution)/shard_map/pallas_call | solution.py:882
  134.1 1.4 %copy.15 = bf16[144,8192]{1,0:T(8,128)(2,1)} copy(bf16[144,8192]{1,0:T(8,128)(2,1)S(1)} %shard_map.127) | data formatting | bytes 4718592

commit v4 on v3

--- a/solution.py
+++ b/solution.py
@@ -14,7 +14,7 @@
 MESH = pl.DeviceIdType.MESH
 F32 = jnp.float32
 BF16 = jnp.bfloat16
-OPS = (6, 1, 0, 1)
+OPS = (5, 0, 1, 1, 3)
 PIECES = (2, 2, 2)
 STACK = 2
 VMEM_LIMIT = 64 * 1024 * 1024 - 4096 * 1024
@@ -377,13 +377,13 @@
     held = rest_refs[9:17]
     gain, bias_query, bias_key, bias_value, near_cos, near_sin, far_cos, far_sin = held
     (
-    gains, small_sem, hid, w_all, wo, acc, kv_all, q_ref, high, total, mixed, att, terms, wo_own,
+    gains, small_sem, hid, w_all, w_second, wo, acc, kv_all, q_ref, high, total, mixed, att, terms, wo_own,
     own_s, own_r, load_sem, swap_s, swap_r, att_s, att_r, ys, yr,
-    ws, wr, wps, wpr, os_, or_, ops, opr, ks, kr, kps, kpr,
+    ws, wr, wps, wpr, os_, or_, ops, opr, ks, kr, kps, kpr, ss, sr, sps, spr,
     ) = rest_refs[17:]
     chips = n // 2
     depth = chips // 2
-    ops_from, ops_first, ops_busy, ops_calm = OPS
+    ops_from, ops_first, ops_busy, ops_calm, ops_gap = OPS
     stack = STACK
     me = lax.axis_index("seq")
     group = lax.axis_index("head")
@@ -410,6 +410,9 @@
     half_depth = w_query.shape[0] // 2
     q_cols = w_query.shape[1]
     heads = q_cols // HEAD_DIM
+    early = heads // 2
+    q_early = early * HEAD_DIM
+    first_cols = 2 * HEAD_DIM + q_early
     out_depth = w_out.shape[0]
     group_cols = w_out.shape[1] // 2
     lane_cols = group_cols // 2
@@ -437,7 +440,8 @@
         slot = w_all.at[2 * me + h]
         loads.append((w_key.at[span], slot.at[:, pl.ds(0, HEAD_DIM)]))
         loads.append((w_value.at[span], slot.at[:, pl.ds(HEAD_DIM, HEAD_DIM)]))
-        loads.append((w_query.at[span], slot.at[:, pl.ds(2 * HEAD_DIM, q_cols)]))
+        loads.append((w_query.at[span, pl.ds(0, q_early)], slot.at[:, pl.ds(2 * HEAD_DIM, q_early)]))
+        last.append((w_query.at[span, pl.ds(q_early, q_cols - q_early)], w_second.at[2 * me + h]))
         last.append((w_out.at[:, wo_lanes(group, h)], wo.at[chip, h, group_rows(group), lanes(core)]))
         last.append((w_out.at[:, wo_lanes(peer, h)], wo_own.at[h, group_rows(group), lanes(core)]))
     copies = [pltpu.make_async_copy(a, b, load_sem.at[i]) for i, (a, b) in enumerate(loads + [(hidden, hid)] + last)]
@@ -577,7 +581,9 @@
     def normed(i):
         line = jnp.concatenate([gains[pl.ds(i * gain_rows + r, 1), :] for r in range(gain_rows)], axis=1)
         scaled = hid[:, columns(i)].astype(F32) * inverse * line
-        return scaled.astype(BF16)
+        value = scaled.astype(BF16)
+        hid[:, columns(i)] = value
+        return value
 
     def widen(line):
         return jnp.broadcast_to(line.astype(F32), (rows, HEAD_DIM))
@@ -588,12 +594,43 @@
     for h in range(heads):
         acc[:, pl.ds((2 + h) * HEAD_DIM, HEAD_DIM)] = widen(lines[h : h + 1])
 
+    far_steps = chips // 2
+    reach = [[far_steps - (j * 2 // parts != d) for j in range(parts)] for d in range(2)]
+
+    def second_copy(owner, send, recv, direction, step, j, device):
+        return remote(w_second.at[2 * owner + j], send, recv, (direction * chips + step) * 2 + j, device)
+
+    def second_begin():
+        for j in range(2):
+            for d in range(2):
+                second_copy(me, ss, sr, d, 0, j, neighbours[d]).start()
+        for j in range(2):
+            second_copy(me, sps, spr, 0, chips - 1, j, partner).start()
+
+    def second_advance(t):
+        for j in range(2):
+            for d in range(2):
+                @pl.when(t < reach[d][j])
+                def _():
+                    owner = source_at(d, t + 1, core)
+                    second_copy(owner, ss, sr, d, t, j, neighbours[d]).wait_recv()
+
+                    @pl.when(t + 1 < reach[d][j])
+                    def _():
+                        second_copy(owner, ss, sr, d, t + 1, j, neighbours[d]).start()
+
+                    second_copy(owner, sps, spr, d, t, j, partner).start()
+
     def project(t, carry):
         @pl.when(t < chips - 1)
         def _():
             for j in range(chunks_in):
                 first.advance(t, j)
 
+        @pl.when(t == chips - 3)
+        def _():
+            second_begin()
+
         @pl.when(t == ops_from)
         def _():
             for d in range(2):
@@ -613,7 +650,7 @@
         for d in range(2):
             i = 2 * source_at(d, t, core) + d
             k = 2 * source_at(d, t, 1 - core) + d
-            acc[...] += jnp.dot(normed(i), w_all[i], preferred_element_type=F32) + jnp.dot(
+            acc[:, pl.ds(0, first_cols)] += jnp.dot(normed(i), w_all[i], preferred_element_type=F32) + jnp.dot(
                 normed(k), w_all[k], preferred_element_type=F32
             )
         return carry
@@ -634,10 +671,10 @@
 
     kv_all[chip, kv_rows(core), pl.ds(0, HEAD_DIM)] = rotary(acc[:, pl.ds(0, HEAD_DIM)]).astype(BF16)
     kv_all[chip, kv_rows(core), pl.ds(HEAD_DIM, HEAD_DIM)] = acc[:, pl.ds(HEAD_DIM, HEAD_DIM)].astype(BF16)
-    q_ref[pl.ds(0, rows), :] = rotary(acc[:, pl.ds(2 * HEAD_DIM, HEAD_DIM)]).astype(BF16)
-
-    far_steps = chips // 2
-    reach = [[far_steps - (j * 2 // parts != d) for j in range(parts)] for d in range(2)]
+    def turn(h):
+        q_ref[pl.ds(h * rows, rows), :] = rotary(acc[:, pl.ds((2 + h) * HEAD_DIM, HEAD_DIM)]).astype(BF16)
+
+    turn(0)
     piece_rows = rows // parts
 
     def kv_copy(owner, send, recv, direction, step, j, device):
@@ -649,13 +686,14 @@
         for d in range(2):
             kv_copy(me, ks, kr, d, 0, j, neighbours[d]).start()
         kv_copy(me, kps, kpr, 0, chips - 1, j, partner).start()
-    for h in range(1, heads):
-        q_ref[pl.ds(h * rows, rows), :] = rotary(acc[:, pl.ds((2 + h) * HEAD_DIM, HEAD_DIM)]).astype(BF16)
+    second_advance(0)
+    for h in range(1, early):
+        turn(h)
 
     factor = HEAD_DIM ** (-0.5) * 1.4426950408889634
 
-    def attend(c, own):
-        for h in range(0, heads, stack):
+    def attend(c, own, which):
+        for h in range(which[0], which[1], stack):
             some = pl.ds(h * rows, stack * rows)
             scores = lax.dot_general(
                 q_ref[some, :], kv_all[c, :, pl.ds(0, HEAD_DIM)], (((1,), (1,)), ((), ())),
@@ -684,11 +722,21 @@
 
     for j in range(parts):
         kv_copy(partner, kps, kpr, 0, chips - 1, j, partner).wait_recv()
-    attend(chip, True)
+    attend(chip, True, (0, early))
 
     busy_steps = far_steps - 1
 
+    def project_second(c):
+        total_part = None
+        for which in range(2):
+            for j in range(2):
+                k = 2 * (2 * c + which) + j
+                value = jnp.dot(hid[:, columns(k)], w_second[k], preferred_element_type=F32)
+                total_part = value if total_part is None else total_part + value
+        acc[:, pl.ds(first_cols, q_cols - q_early)] += total_part
+
     def attention(t, carry):
+        second_advance(t + 1)
         for j in range(parts):
             for d in range(2):
                 @pl.when(t < reach[d][j])
@@ -715,17 +763,43 @@
                 def _():
                     owner = source_at(d, t, 1 - core)
                     kv_copy(owner, kps, kpr, d, t - 1, j, partner).wait_recv()
+                    second_copy(owner, sps, spr, d, t - 1, j, partner).wait_recv()
+
+        @pl.when(t == 0)
+        def _():
+            for j in range(2):
+                second_copy(partner, sps, spr, 0, chips - 1, j, partner).wait_recv()
 
         for d in range(2):
             other = source_at(d, t, core) // 2
 
             @pl.when((t > 0) & (t <= far_steps - d) & (other < chip))
             def _():
-                attend(other, False)
+                attend(other, False, (0, early))
+
+            @pl.when(((t > 0) | (d == 0)) & (t <= far_steps - d))
+            def _():
+                project_second(other)
         return carry
 
     lax.fori_loop(0, far_steps + 1, attention, 0)
-    ops_done = ops_first + ops_busy * busy_steps + ops_calm * (far_steps + 1 - busy_steps)
+    ops_middle = ops_first + ops_busy * busy_steps + ops_calm * (far_steps + 1 - busy_steps)
+    ops_done = ops_middle + (chips + ops_gap - 1) // ops_gap
+    for h in range(early, heads):
+        turn(h)
+    attend(chip, True, (early, heads))
+
+    def attention_rest(c, carry):
+        @pl.when(c % ops_gap == 0)
+        def _():
+            third.op(ops_middle + c // ops_gap)
+
+        @pl.when(c < chip)
+        def _():
+            attend(c, False, (early, heads))
+        return carry
+
+    lax.fori_loop(0, chips, attention_rest, 0)
 
     def row_span(which):
         return pl.ds(pl.multiple_of(which * rh, rh), rh)
@@ -837,7 +911,10 @@
             for t in range(reach[d][j]):
                 kv_copy(me, ks, kr, d, t, j, neighbours[d]).wait_send()
                 kv_copy(me, kps, kpr, d, t, j, partner).wait_send()
+                second_copy(me, ss, sr, d, t, j, neighbours[d]).wait_send()
+                second_copy(me, sps, spr, d, t, j, partner).wait_send()
         kv_copy(me, kps, kpr, 0, chips - 1, j, partner).wait_send()
+        second_copy(me, sps, spr, 0, chips - 1, j, partner).wait_send()
     for d in range(2):
         swap(d).wait_send()
         swap_own(d).wait_send()
@@ -869,6 +946,7 @@
     rows, width = hidden.shape
     cols = w_query.shape[1]
     heads = cols // HEAD_DIM
+    early = heads // 2 * HEAD_DIM
     chips = n // 2
     slices = 2 * n
     half_depth = w_query.shape[0] // 2
@@ -889,7 +967,8 @@
             pltpu.VMEM((width // HEAD_DIM, HEAD_DIM), F32),
             dma((8,)),
             pltpu.VMEM((rows, width), BF16),
-            pltpu.VMEM((slices, half_depth, 2 * HEAD_DIM + cols), BF16),
+            pltpu.VMEM((slices, half_depth, 2 * HEAD_DIM + early), BF16),
+            pltpu.VMEM((slices, half_depth, cols - early), BF16),
             pltpu.VMEM((chips, 2, 2 * w_out.shape[0], group_cols), BF16),
             pltpu.VMEM((rows, 2 * HEAD_DIM + cols), F32),
             pltpu.VMEM((chips, 2 * rows, 2 * HEAD_DIM), BF16),
@@ -901,13 +980,14 @@
             pltpu.VMEM((chips, 2, rows // 2, group_cols), BF16),
             pltpu.VMEM((2, 2 * w_out.shape[0], group_cols), BF16),
             dma((2,)), dma((2,)),
-            dma((11,)),
+            dma((13,)),
             dma((4,)), dma((4,)), dma((2,)), dma((2,)),
             dma((4 * chips,)), dma((4 * chips,)),
         ]
         + [dma((2 * chips * chunks_in,))] * 4
         + [dma((2 * chips * chunks_out,))] * 4
-        + [dma((2 * chips * parts,))] * 4,
+        + [dma((2 * chips * parts,))] * 4
+        + [dma((4 * chips,))] * 4,
         compiler_params=pltpu.CompilerParams(
             collective_id=0, has_side_effects=True, vmem_limit_bytes=VMEM_LIMIT - 2 * result.size
         ),
@@ -920,7 +1000,7 @@
         groups == 2
         and chips % 4 == 0
         and rows % 32 == 0
-        and w_query.shape[1] % HEAD_DIM == 0
+        and w_query.shape[1] % (4 * HEAD_DIM) == 0
         and w_query.shape[0] % 128 == 0
         and w_out.shape[1] % 512 == 0
     )

time: 136 us -> 134 us (0.985)
  Pallas kernels: 134 us -> 132 us
    pallas_call x1, Pallas kernels: 134 us -> 132 us  [pair_local(): pl.pallas_call(functools.partial(pair_kernel, n, chunks_in, chunks_out, p...]
where the time goes in v4:
time: 134 us
  Pallas kernels  132 us (99%)
  local copies, waits for them, and re-layouts  1.41 us (1%)
    pallas_call x1, Pallas kernels, pair_local(): pl.pallas_call(functools.partial(pair_kernel, n, chunks_in, chunks_out, p...  132 us

profile of v4, /device:TPU:0, one launch (start us, length us, event | category | flops | bytes accessed | tf_op | source)
XLA Modules:
  0.0 133.7 jit_solution(2145174884513344670)
XLA Ops:
  0.0 132.3 %shard_map.127 = bf16[144,8192]{1,0:T(8,128)(2,1)S(1)} custom-call(bf16[288,8192]{1,0:T(8,128)(2,1)} %hidden.1, bf16[512,512]{1,0:T(8,128)(2,1)} %w_query.1, bf16[512,128]{1,0:T(8,128)(2,1)} %w_key.1, bf16[512,128]{1,0:T(8,128)(2,1)} %w_value.1, bf16[512,512]{1,0:T(8,128)(2,1)} %w_out.1, bf16[64,128]{1,0:T(8,128)(2,1)} %bitcast.4, bf16[4,128]{1,0:T(4,128)(2,1)} %bitcast.5, ...), custom_call_target="tpu_custom_call" | custom-call | tf_op jit(solution)/shard_map/pallas_call | solution.py:960
  132.3 1.4 %copy.15 = bf16[144,8192]{1,0:T(8,128)(2,1)} copy(bf16[144,8192]{1,0:T(8,128)(2,1)S(1)} %shard_map.127) | data formatting | bytes 4718592

commit v5 on v4

--- a/solution.py
+++ b/solution.py
@@ -873,13 +873,14 @@
         for d in range(2):
             give(t, d)
 
+        move(chunks_out - 1)
+
         @pl.when(t == 1)
         def _():
             att_copy(1).wait_recv()
 
         for d in range(2):
             keep(t, d)
-        move(chunks_out - 1)
 
         @pl.when(t == chips // 2)
         def _():

time: 134 us -> 135 us (level)
  no operation moved by 1% of the time
where the time goes in v5:
time: 135 us
  Pallas kernels  133 us (99%)
  local copies, waits for them, and re-layouts  1.41 us (1%)
    pallas_call x1, Pallas kernels, pair_local(): pl.pallas_call(functools.partial(pair_kernel, n, chunks_in, chunks_out, p...  133 us

profile of v5, /device:TPU:0, one launch (start us, length us, event | category | flops | bytes accessed | tf_op | source)
XLA Modules:
  0.0 134.8 jit_solution(15787184335616025484)
XLA Ops:
  0.0 133.3 %shard_map.127 = bf16[144,8192]{1,0:T(8,128)(2,1)S(1)} custom-call(bf16[288,8192]{1,0:T(8,128)(2,1)} %hidden.1, bf16[512,512]{1,0:T(8,128)(2,1)} %w_query.1, bf16[512,128]{1,0:T(8,128)(2,1)} %w_key.1, bf16[512,128]{1,0:T(8,128)(2,1)} %w_value.1, bf16[512,512]{1,0:T(8,128)(2,1)} %w_out.1, bf16[64,128]{1,0:T(8,128)(2,1)} %bitcast.4, bf16[4,128]{1,0:T(4,128)(2,1)} %bitcast.5, ...), custom_call_target="tpu_custom_call" | custom-call | tf_op jit(solution)/shard_map/pallas_call | solution.py:961
  133.4 1.4 %copy.15 = bf16[144,8192]{1,0:T(8,128)(2,1)} copy(bf16[144,8192]{1,0:T(8,128)(2,1)S(1)} %shard_map.127) | data formatting | bytes 4718592
